TPU v7x, 32 devices: a whole 2x2x4 slice. The times are simulated.
32 devices in a mesh: wide: 4 (over x, core), narrow: 8 (over z, y).
Axes of the slice: x: 2, y: 2, z: 4, core: 2. Of those that a mesh axis runs over, the one named last changes fastest.
Arguments:
- velocity: float32 [3, 1, 4096, 4096], P(None, None, ('wide', 'narrow')), may hold values from -6 to 6
- plane_wavenumber: float32 [1], replicated, may hold values from 2 to 1024
Outputs:
- projected: float32 [3, 1, 4096, 4096], P(None, None, ('wide', 'narrow'))
All inputs are finite; a program needn't handle non-finite values.
Results may differ from a plain program's by a relative error of at most 0.00007.
Values sent between devices are 32-bit elements; how exact they have to be, the bound alone decides.
No kernel may reach another device: no remote copies, remote signals or barrier semaphores. Data moves between devices by JAX's collectives and lax.ppermute only.
A program may use at most 128 MiB of HBM per device.

v0:
```python
import math

import jax
import jax.numpy as jnp
from jax import lax
from jax.sharding import PartitionSpec as P

radix_split = 64
highest = lax.Precision.HIGHEST


def angle_tables(row_size, col_size, period, direction):
    product = jnp.arange(row_size)[:, None] * jnp.arange(col_size)[None, :] % period
    angles = direction * 2.0 * math.pi * product.astype(jnp.float32) / period
    return (jnp.cos(angles), jnp.sin(angles))


def complex_product(pattern, left_real, left_imag, table_real, table_imag):
    out_real = jnp.einsum(pattern, left_real, table_real, precision=highest) - jnp.einsum(
        pattern, left_imag, table_imag, precision=highest
    )
    out_imag = jnp.einsum(pattern, left_real, table_imag, precision=highest) + jnp.einsum(
        pattern, left_imag, table_real, precision=highest
    )
    return (out_real, out_imag)


def transform(real_part, imag_part, direction):
    length = real_part.shape[-1]
    inner_size = length // radix_split
    leading = real_part.shape[:-1]
    grid_real = real_part.reshape(leading + (radix_split, inner_size))
    grid_imag = imag_part.reshape(leading + (radix_split, inner_size))
    outer_cos, outer_sin = angle_tables(radix_split, radix_split, radix_split, direction)
    section_real, section_imag = complex_product(
        "...ab,ak->...kb", grid_real, grid_imag, outer_cos, outer_sin
    )
    twist_cos, twist_sin = angle_tables(radix_split, inner_size, length, direction)
    turned_real = section_real * twist_cos - section_imag * twist_sin
    turned_imag = section_real * twist_sin + section_imag * twist_cos
    inner_cos, inner_sin = angle_tables(inner_size, inner_size, inner_size, direction)
    final_real, final_imag = complex_product(
        "...kb,bm->...mk", turned_real, turned_imag, inner_cos, inner_sin
    )
    return (final_real.reshape(leading + (length,)), final_imag.reshape(leading + (length,)))


def project(lines, wave_x, wave_z, kept_line):
    groups, per_device, length_y = lines.shape
    shaped = lines.reshape(3, 2, groups // 6, per_device, length_y)
    spec_real, spec_imag = transform(shaped[:, 0], shaped[:, 1], -1.0)
    index_y = jnp.arange(length_y)
    signed_y = jnp.where(index_y <= length_y // 2, index_y, index_y - length_y)
    kept_y = jnp.abs(signed_y) <= length_y // 3
    retained = (kept_line & kept_y[None, None, :]).astype(jnp.float32)
    wave_y = signed_y.astype(jnp.float32)[None, None, :]
    wave_square = wave_x * wave_x + wave_y * wave_y + wave_z * wave_z
    waves = (wave_x, wave_y, wave_z)
    div_real = wave_x * spec_real[0] + wave_y * spec_real[1] + wave_z * spec_real[2]
    div_imag = wave_x * spec_imag[0] + wave_y * spec_imag[1] + wave_z * spec_imag[2]
    proj_real = jnp.stack(
        [
            (spec_real[component] - waves[component] * div_real / wave_square) * retained
            for component in range(3)
        ]
    )
    proj_imag = jnp.stack(
        [
            (spec_imag[component] - waves[component] * div_imag / wave_square) * retained
            for component in range(3)
        ]
    )
    back_real, back_imag = transform(proj_real, proj_imag, 1.0)
    return jnp.stack([back_real / length_y, back_imag / length_y], axis=1).reshape(
        groups, per_device, length_y
    )


def first_send(spectrum, first_size):
    groups, rows, span = spectrum.shape
    return (
        spectrum.reshape(groups, rows, first_size, span // first_size)
        .transpose(2, 0, 1, 3)
        .reshape(first_size, 1, -1)
    )


def second_send(received, first_size, second_size, groups, rows, per_device):
    shaped = received.reshape(first_size, groups, rows, second_size, per_device)
    return shaped.transpose(3, 1, 4, 0, 2).reshape(second_size, 1, -1)


def arrange_lines(received, first_size, second_size, groups, rows, per_device):
    shaped = received.reshape(second_size, groups, per_device, first_size, rows)
    ordered = shaped.transpose(1, 2, 0, 3, 4)
    return ordered.reshape(groups, per_device, -1)


def first_return(solved, first_size, second_size, rows):
    groups, per_device, _ = solved.shape
    shaped = solved.reshape(groups, per_device, second_size, first_size, rows).transpose(
        2, 0, 1, 3, 4
    )
    return shaped.reshape(second_size, 1, -1)


def second_return(received, first_size, second_size, groups, rows, per_device):
    shaped = received.reshape(second_size, groups, per_device, first_size, rows)
    return shaped.transpose(3, 1, 4, 0, 2).reshape(first_size, 1, -1)


def arrange_rows(received, first_size, groups, rows):
    shaped = received.reshape(first_size, groups, rows, -1)
    return shaped.transpose(1, 2, 0, 3).reshape(groups, rows, -1)


def local(velocity, plane_wavenumber):
    components, plane_count, row_count, x_length = velocity.shape
    wide_size = lax.axis_size("wide")
    narrow_size = lax.axis_size("narrow")
    device_count = wide_size * narrow_size
    keep_x = x_length // 3 + 1
    spec_real, spec_imag = transform(velocity, jnp.zeros_like(velocity), -1.0)
    spec_real = spec_real[..., :keep_x]
    spec_imag = spec_imag[..., :keep_x]
    per_device = (keep_x + device_count - 1) // device_count
    line_span = per_device * device_count
    gap = ((0, 0), (0, 0), (0, 0), (0, 0), (0, line_span - keep_x))
    stacked = jnp.stack([spec_real, spec_imag], axis=1)
    spectrum = jnp.pad(stacked, gap).reshape(components * 2 * plane_count, row_count, line_span)
    groups = spectrum.shape[0]
    halfway = lax.all_to_all(
        first_send(spectrum, narrow_size), "narrow", split_axis=0, concat_axis=1, tiled=True
    )
    outgoing = second_send(halfway, narrow_size, wide_size, groups, row_count, per_device)
    arrived = lax.all_to_all(outgoing, "wide", split_axis=0, concat_axis=1, tiled=True)
    lines = arrange_lines(arrived, narrow_size, wide_size, groups, row_count, per_device)
    line_start = (
        lax.axis_index("narrow") * (per_device * wide_size) + lax.axis_index("wide") * per_device
    )
    indices = line_start + jnp.arange(per_device)
    wave_x = indices.astype(jnp.float32)[None, :, None]
    wave_z = plane_wavenumber[:, None, None]
    kept_line = (indices < keep_x)[None, :, None]
    solved = project(lines, wave_x, wave_z, kept_line)
    halfway = lax.all_to_all(
        first_return(solved, narrow_size, wide_size, row_count),
        "wide",
        split_axis=0,
        concat_axis=1,
        tiled=True,
    )
    outgoing = second_return(halfway, narrow_size, wide_size, groups, row_count, per_device)
    arrived = lax.all_to_all(outgoing, "narrow", split_axis=0, concat_axis=1, tiled=True)
    returned = arrange_rows(arrived, narrow_size, groups, row_count)
    columns = returned.reshape(components, 2, plane_count, row_count, line_span)[..., :keep_x]
    weights = jnp.where(jnp.arange(keep_x) == 0, 1.0, 2.0).astype(jnp.float32)
    widen = ((0, 0), (0, 0), (0, 0), (0, x_length - keep_x))
    back_real = jnp.pad(columns[:, 0] * weights, widen)
    back_imag = jnp.pad(columns[:, 1] * weights, widen)
    out_real, out_imag = transform(back_real, back_imag, 1.0)
    return out_real / x_length


def solution(mesh):
    placed = (P(None, None, ("wide", "narrow"), None), P())
    return jax.shard_map(
        local,
        mesh=mesh,
        in_specs=placed,
        out_specs=P(None, None, ("wide", "narrow"), None),
        check_vma=False,
    )
```

profile of v0, /device:TPU:0, one launch (start us, length us, event | category | flops | bytes accessed | tf_op | source)
XLA Modules:
  0.0 851.3 jit_solution(1181814289955283655)
XLA Ops:
  0.1 4.6 fusion.52
  4.8 4.7 fusion.54
  9.5 6.6 copy.55
  16.1 13.6 %fusion.28 = f32[64,3,128,64]{2,0,3,1:T(8,128)} fusion(f32[3,128,64,64]{1,3,2,0:T(8,128)} %bitcast.346), kind=kOutput, calls=%fused_computation.39 | convolution fusion | flops 1208016896 | bytes 12582912 | tf_op jit(solution)/shard_map/...ab,ak->...kb/dot_general | solution.py:22
  29.7 19.1 %fusion.5 = (f32[3,128,64,64]{1,2,3,0:T(8,128)}, f32[3,128,64,64]{1,2,3,0:T(8,128)S(1)}) fusion(f32[64,64]{0,1:T(8,128)S(1)} %get-tuple-element.25, f32[64,64]{0,1:T(8,128)S(1)} %get-tuple-element.26, f32[64,3,128,64]{2,0,3,1:T(8,128)} %fusion.28, f32[64,3,128,64]{2,0,3,1:T(8,128)} %fusion.52, f32[64,3,128,64]{2,0,3,1:T(8,128)} %fusion.54, ...), kind=kOutput, calls=%fused_computation.11 | convolution fusion | flops 1220599808 | bytes 37781504 | tf_op jit(solution)/shard_map/...ab,ak->...kb/dot_general | solution.py:19
  48.8 9.5 %fusion.22 = f32[64,3,128,64]{2,0,3,1:T(8,128)S(1)} fusion(f32[3,128,64,64]{1,2,3,0:T(8,128)S(1)} %get-tuple-element.12), kind=kOutput, calls=%fused_computation.33 | convolution fusion | flops 1208016896 | bytes 12582912 | tf_op jit(solution)/shard_map/...kb,bm->...mk/dot_general | solution.py:19
  58.3 9.6 %fusion.20 = f32[64,3,128,64]{2,0,3,1:T(8,128)S(1)} fusion(f32[3,128,64,64]{1,2,3,0:T(8,128)S(1)} %get-tuple-element.12), kind=kOutput, calls=%fused_computation.31 | convolution fusion | flops 1208016896 | bytes 12582912 | tf_op jit(solution)/shard_map/...kb,bm->...mk/dot_general | solution.py:22
  68.0 9.7 %subtract_bitcast_fusion = f32[3,1,128,64,64]{2,3,4,0,1:T(8,128)S(1)} fusion(f32[64,3,128,64]{2,0,3,1:T(8,128)S(1)} %fusion.22, f32[3,128,64,64]{1,2,3,0:T(8,128)S(1)} %bitcast.349), kind=kOutput, calls=%fused_computation.22 | convolution fusion | flops 1209589760 | bytes 18874368 | tf_op jit(solution)/shard_map/...kb,bm->...mk/dot_general | solution.py:19
  77.8 3.6 copy.60
  81.5 10.0 %add_bitcast_fusion = f32[3,1,128,64,64]{2,3,4,0,1:T(8,128)S(1)} fusion(f32[64,3,128,64]{2,0,3,1:T(8,128)S(1)} %fusion.20, f32[3,128,64,64]{1,2,3,0:T(8,128)S(1)} %bitcast.349), kind=kOutput, calls=%fused_computation.21 | convolution fusion | flops 1209589760 | bytes 18874368 | tf_op jit(solution)/shard_map/...kb,bm->...mk/dot_general | solution.py:22
  91.5 3.6 copy.63
  98.2 4.8 reshape_reshape.12
  102.9 6.1 copy.65
  109.1 12.0 %reshape.976 = f32[8,1,132096]{2,1,0:T(1,128)} reshape(f32[8,6,128,172]{3,2,1,0:T(8,128)} %copy.65) | data formatting | bytes 8454144 | tf_op jit(solution)/shard_map/reshape | solution.py:84
  121.0 102.0 %all_to_all.16 = f32[8,1,132096]{2,1,0:T(1,128)} all-to-all(f32[8,1,132096]{2,1,0:T(1,128)} %reshape.976), channel_id=1, replica_groups=mesh['wide'=4,'narrow'=8] {'narrow'}, dimensions={0} | all-to-all | bytes 8454144 | tf_op jit(solution)/shard_map/all_to_all | solution.py:132
  223.0 13.4 %reduce = f32[8,132096]{1,0:T(8,128)} reduce(f32[8,1,132096]{2,1,0:T(1,128)} %all_to_all.16, f32[]{:T(128)} %constant.129), dimensions={1}, to_apply=%all_to_all.8.reduce_sub_computation | reduce | bytes 8454148 | tf_op jit(solution)/shard_map/all_to_all | solution.py:132
  236.4 26.8 %reshape.953 = f32[8,6,128,4,43]{4,3,2,1,0:T(4,128)} reshape(f32[8,132096]{1,0:T(8,128)} %reduce) | data formatting | bytes 8454144 | tf_op jit(solution)/shard_map/reshape | solution.py:89
  263.2 9.2 %copy.67 = f32[4,6,43,8,128]{4,3,2,1,0:T(8,128)} copy(f32[4,6,43,8,128]{2,0,4,1,3:T(4,128)} %bitcast.354) | data formatting | bytes 8454144 | tf_op jit(solution)/shard_map/transpose | solution.py:90
  272.5 5.1 all-to-all-start.1
  279.0 47.0 %all-to-all-done.1 = f32[4,1,264192]{2,1,0:T(1,128)} async-done(((f32[4,1,264192]{2,1,0:T(1,128)}), f32[4,1,264192]{2,1,0:T(1,128)}, u32[]{:S(2)}, u32[]{:S(2)}) %all-to-all-start.1) | async-done | bytes 4227104 | tf_op jit(solution)/shard_map/all_to_all | solution.py:136
  326.1 4.8 copy.134
  330.9 5.8 reshape_reshape.13
  336.7 9.3 %fusion.259 = (f32[3,1,1,43,4096]{4,1,0,3,2:T(1,128)}, f32[3,1,1,43,4096]{4,1,0,3,2:T(1,128)S(1)}) fusion(f32[3,2,1,43,4096]{4,1,0,3,2:T(2,128)} %reshape_reshape.13), kind=kLoop, calls=%fused_computation.298 | loop fusion | bytes 8454144 | tf_op jit(solution)/shard_map/slice | solution.py:51
  347.8 3.7 reshape.956
  351.5 8.2 fusion.107
  359.7 6.0 fusion.97
  367.4 3.6 reshape.957
  371.0 7.9 convolution_subtract_fusion
  379.0 4.4 convolution_add_fusion
  383.4 11.3 %fusion.42 = f32[64,3,43,64]{3,0,2,1:T(8,128)S(1)} fusion(f32[64,3,43,64]{3,0,2,1:T(8,128)S(1)} %convolution_add_fusion, f32[64,3,43,64]{3,0,2,1:T(8,128)S(1)} %convolution_subtract_fusion, f32[64,64]{1,0:T(8,128)S(1)} %copy.73, f32[64,64]{1,0:T(8,128)S(1)} %copy.72), kind=kOutput, calls=%fused_computation.60 | convolution fusion | flops 407441408 | bytes 6373376 | tf_op jit(solution)/shard_map/...kb,bm->...mk/dot_general | solution.py:22
  394.8 11.5 %fusion.44 = f32[64,3,43,64]{3,0,2,1:T(8,128)S(1)} fusion(f32[64,3,43,64]{3,0,2,1:T(8,128)S(1)} %convolution_add_fusion, f32[64,3,43,64]{3,0,2,1:T(8,128)S(1)} %convolution_subtract_fusion, f32[64,64]{1,0:T(8,128)S(1)} %copy.73, f32[64,64]{1,0:T(8,128)S(1)} %copy.72), kind=kOutput, calls=%fused_computation.62 | convolution fusion | flops 407441408 | bytes 6373376 | tf_op jit(solution)/shard_map/...kb,bm->...mk/dot_general | solution.py:19
  406.3 11.1 %add_bitcast_fusion.1 = f32[3,1,43,64,64]{4,3,2,0,1:T(8,128)S(1)} fusion(f32[64,3,43,64]{3,0,2,1:T(8,128)S(1)} %fusion.42, f32[64,3,43,64]{3,0,2,1:T(8,128)S(1)} %convolution_add_fusion, f32[64,3,43,64]{3,0,2,1:T(8,128)S(1)} %convolution_subtract_fusion, f32[64,64]{1,0:T(8,128)S(1)} %copy.73, f32[64,64]{1,0:T(8,128)S(1)} %copy.72), kind=kOutput, calls=%fused_computation.77 | convolution fusion | flops 407969792 | bytes 8486912 | tf_op jit(solution)/shard_map/...kb,bm->...mk/dot_general | solution.py:22
  417.4 11.3 %subtract_bitcast_fusion.1 = f32[3,1,43,64,64]{4,3,2,0,1:T(8,128)S(1)} fusion(f32[64,3,43,64]{3,0,2,1:T(8,128)S(1)} %fusion.44, f32[64,3,43,64]{3,0,2,1:T(8,128)S(1)} %convolution_add_fusion, f32[64,3,43,64]{3,0,2,1:T(8,128)S(1)} %convolution_subtract_fusion, f32[64,64]{1,0:T(8,128)S(1)} %copy.73, f32[64,64]{1,0:T(8,128)S(1)} %copy.72), kind=kOutput, calls=%fused_computation.78 | convolution fusion | flops 407969792 | bytes 8486912 | tf_op jit(solution)/shard_map/...kb,bm->...mk/dot_general | solution.py:19
  432.0 4.3 fusion.57
  436.3 4.0 fusion.56
  440.3 4.8 fusion.66
  445.1 4.5 fusion.67
  449.6 11.3 %fusion.34 = f32[64,3,43,64]{3,0,2,1:T(8,128)S(1)} fusion(f32[64,3,43,64]{3,0,2,1:T(8,128)S(1)} %fusion.67, f32[64,3,43,64]{3,0,2,1:T(8,128)S(1)} %fusion.66, f32[64,64]{1,0:T(8,128)S(1)} %copy.77, f32[64,64]{1,0:T(8,128)S(1)} %copy.76), kind=kOutput, calls=%fused_computation.48 | convolution fusion | flops 407441408 | bytes 6373376 | tf_op jit(solution)/shard_map/...kb,bm->...mk/dot_general | solution.py:19
  460.9 13.1 %fusion.32 = f32[64,3,43,64]{3,0,2,1:T(8,128)} fusion(f32[64,3,43,64]{3,0,2,1:T(8,128)S(1)} %fusion.67, f32[64,3,43,64]{3,0,2,1:T(8,128)S(1)} %fusion.66, f32[64,64]{1,0:T(8,128)S(1)} %copy.77, f32[64,64]{1,0:T(8,128)S(1)} %copy.76), kind=kOutput, calls=%fused_computation.46 | convolution fusion | flops 407441408 | bytes 6373376 | tf_op jit(solution)/shard_map/...kb,bm->...mk/dot_general | solution.py:22
  473.9 13.3 %multiply_bitcast_fusion.2 = f32[3,1,43,64,64]{4,3,2,0,1:T(8,128)} fusion(f32[64,3,43,64]{3,0,2,1:T(8,128)S(1)} %fusion.34, f32[64,3,43,64]{3,0,2,1:T(8,128)S(1)} %fusion.67, f32[64,3,43,64]{3,0,2,1:T(8,128)S(1)} %fusion.66, f32[64,64]{1,0:T(8,128)S(1)} %copy.77, f32[64,64]{1,0:T(8,128)S(1)} %copy.76), kind=kOutput, calls=%fused_computation.76 | convolution fusion | flops 408498176 | bytes 8486912 | tf_op jit(solution)/shard_map/...kb,bm->...mk/dot_general | solution.py:19
  487.3 5.0 div.201
  492.3 17.7 %multiply_bitcast_fusion.1 = f32[3,1,43,64,64]{4,3,2,0,1:T(8,128)} fusion(f32[64,3,43,64]{3,0,2,1:T(8,128)} %fusion.32, f32[64,3,43,64]{3,0,2,1:T(8,128)} %copy-done.1, f32[64,3,43,64]{3,0,2,1:T(8,128)} %copy-done, f32[64,64]{1,0:T(8,128)S(1)} %copy.77, f32[64,64]{1,0:T(8,128)S(1)} %copy.76), kind=kOutput, calls=%fused_computation.75 | convolution fusion | flops 408498176 | bytes 8486912 | tf_op jit(solution)/shard_map/...kb,bm->...mk/dot_general | solution.py:22
  510.0 5.7 div.205
  515.7 5.9 pad_maximum_fusion
  521.5 3.7 copy.78
  525.2 6.7 reshape_reshape.14
  534.3 52.0 %all_to_all.17 = f32[4,1,264192]{2,1,0:T(1,128)} all-to-all(f32[4,1,264192]{2,1,0:T(1,128)S(1)} %bitcast.365), channel_id=1, replica_groups=mesh['wide'=4,'narrow'=8] {'wide'}, dimensions={0} | all-to-all | bytes 8454144 | tf_op jit(solution)/shard_map/all_to_all | solution.py:146
  586.3 9.0 %copy.81 = f32[4,6,43,8,128]{2,0,4,1,3:T(4,128)} copy(f32[4,6,43,8,128]{4,3,2,1,0:T(8,128)} %bitcast.367) | data formatting | bytes 8454144 | tf_op jit(solution)/shard_map/reshape | solution.py:108
  595.3 20.3 %reshape.977 = f32[8,1,132096]{2,1,0:T(1,128)} reshape(f32[8,6,128,4,43]{4,3,2,1,0:T(4,128)} %bitcast.355) | data formatting | bytes 8454144 | tf_op jit(solution)/shard_map/reshape | solution.py:109
  615.5 4.8 all-to-all-start.3
  620.4 94.2 %all-to-all-done.3 = f32[8,1,132096]{2,1,0:T(1,128)} async-done(((f32[8,1,132096]{2,1,0:T(1,128)}), f32[8,1,132096]{2,1,0:T(1,128)}, u32[]{:S(2)}, u32[]{:S(2)}) %all-to-all-start.3) | async-done | bytes 4227104 | tf_op jit(solution)/shard_map/all_to_all | solution.py:154
  714.6 13.2 %reduce.1 = f32[8,132096]{1,0:T(8,128)} reduce(f32[8,1,132096]{2,1,0:T(1,128)} %all-to-all-done.3, f32[]{:T(128)} %constant.129), dimensions={1}, to_apply=%all_to_all.11.reduce_sub_computation | reduce | bytes 8454148 | tf_op jit(solution)/shard_map/all_to_all | solution.py:154
  727.8 13.7 %reshape.967 = f32[8,6,128,172]{3,2,1,0:T(8,128)} reshape(f32[8,132096]{1,0:T(8,128)} %reduce.1) | data formatting | bytes 8454144 | tf_op jit(solution)/shard_map/reshape | solution.py:113
  741.5 6.0 copy.83
  747.5 4.8 reshape_reshape.15
  752.3 2.6 fusion.76
  755.3 13.5 %fusion.12 = f32[64,3,128,64]{2,0,3,1:T(8,128)} fusion(f32[3,128,64,64]{1,3,2,0:T(8,128)S(1)} %bitcast.352), kind=kOutput, calls=%fused_computation.23 | convolution fusion | flops 1208016896 | bytes 12582912 | tf_op jit(solution)/shard_map/...ab,ak->...kb/dot_general | solution.py:22
  768.8 13.0 %fusion.14 = f32[64,3,128,64]{2,0,3,1:T(8,128)} fusion(f32[3,128,64,64]{1,3,2,0:T(8,128)S(1)} %bitcast.353), kind=kOutput, calls=%fused_computation.25 | convolution fusion | flops 1208016896 | bytes 12582912 | tf_op jit(solution)/shard_map/...ab,ak->...kb/dot_general | solution.py:19
  782.1 13.2 %fusion.16 = f32[64,3,128,64]{2,0,3,1:T(8,128)} fusion(f32[3,128,64,64]{1,3,2,0:T(8,128)S(1)} %bitcast.350), kind=kOutput, calls=%fused_computation.27 | convolution fusion | flops 1208016896 | bytes 12582912 | tf_op jit(solution)/shard_map/...ab,ak->...kb/dot_general | solution.py:22
  795.3 19.8 %fusion.1 = (f32[3,128,64,64]{1,2,3,0:T(8,128)}, f32[3,128,64,64]{1,2,3,0:T(8,128)}) fusion(f32[64,64]{0,1:T(8,128)S(1)} %get-tuple-element.27, f32[64,64]{0,1:T(8,128)S(1)} %get-tuple-element.28, f32[64,3,128,64]{2,0,3,1:T(8,128)} %fusion.16, f32[64,3,128,64]{2,0,3,1:T(8,128)} %fusion.12, f32[64,3,128,64]{2,0,3,1:T(8,128)} %fusion.14, ...), kind=kOutput, calls=%fused_computation.3 | convolution fusion | flops 1220599808 | bytes 37781504 | tf_op jit(solution)/shard_map/...ab,ak->...kb/dot_general | solution.py:19
  815.2 12.6 %fusion.8 = f32[64,3,128,64]{2,0,3,1:T(8,128)S(1)} fusion(f32[3,128,64,64]{1,2,3,0:T(8,128)} %get-tuple-element.10), kind=kOutput, calls=%fused_computation.16 | convolution fusion | flops 1208016896 | bytes 12582912 | tf_op jit(solution)/shard_map/...kb,bm->...mk/dot_general | solution.py:19
  827.8 10.2 %multiply_bitcast_fusion = f32[3,1,128,64,64]{2,3,4,0,1:T(8,128)S(1)} fusion(f32[64,3,128,64]{2,0,3,1:T(8,128)S(1)} %fusion.8, f32[3,128,64,64]{1,2,3,0:T(8,128)S(1)} %bitcast.357), kind=kOutput, calls=%fused_computation.20 | convolution fusion | flops 1211162624 | bytes 18874368 | tf_op jit(solution)/shard_map/...kb,bm->...mk/dot_general | solution.py:19
  838.0 6.3 copy.91
  844.3 6.6 copy.92
  (53 shorter events, 14.1 us)
Async XLA Ops:
  48.8 19.2 %slice-start = ((s8[6291456]{0:T(1024)(128)(4,1)}), s8[4194304]{0:T(1024)(128)(4,1)S(1)}, s32[]{:S(2)}) async-start(s8[6291456]{0:T(1024)(128)(4,1)} %bitcast.348), calls=%async_computation.4 | async-start | bytes 8388608
  58.3 9.7 %slice-start.1 = ((s8[6291456]{0:T(1024)(128)(4,1)}), s8[2097152]{0:T(1024)(128)(4,1)S(1)}, s32[]{:S(2)}) async-start(s8[6291456]{0:T(1024)(128)(4,1)} %bitcast.348), calls=%async_computation.5 | async-start | bytes 4194304
  272.5 53.6 %all-to-all-start.1 = ((f32[4,1,264192]{2,1,0:T(1,128)}), f32[4,1,264192]{2,1,0:T(1,128)}, u32[]{:S(2)}, u32[]{:S(2)}) async-start(f32[4,1,264192]{2,1,0:T(1,128)} %bitcast.366), calls=%async_computation.1 | async-start | bytes 8454144 | tf_op jit(solution)/shard_map/all_to_all | solution.py:136
  351.5 8.2 copy-start.3
  359.7 6.0 copy-start.4
  367.4 11.6 %slice-start.4 = ((s8[4227072]{0:T(1024)(128)(4,1)}), s8[32768]{0:T(1024)(128)(4,1)S(1)}, s32[]{:S(2)}) async-start(s8[4227072]{0:T(1024)(128)(4,1)} %bitcast.361), calls=%async_computation.8 | async-start | bytes 65536
  371.0 8.0 copy-start.2
  371.0 8.0 slice-start.5
  445.1 28.9 %copy-start = (f32[64,3,43,64]{3,0,2,1:T(8,128)}, f32[64,3,43,64]{3,0,2,1:T(8,128)S(1)}, u32[]{:S(2)}) copy-start(f32[64,3,43,64]{3,0,2,1:T(8,128)S(1)} %fusion.66) | copy-start | bytes 6340612
  449.6 24.4 %copy-start.1 = (f32[64,3,43,64]{3,0,2,1:T(8,128)}, f32[64,3,43,64]{3,0,2,1:T(8,128)S(1)}, u32[]{:S(2)}) copy-start(f32[64,3,43,64]{3,0,2,1:T(8,128)S(1)} %fusion.67) | copy-start | bytes 6340612
  615.5 99.0 %all-to-all-start.3 = ((f32[8,1,132096]{2,1,0:T(1,128)}), f32[8,1,132096]{2,1,0:T(1,128)}, u32[]{:S(2)}, u32[]{:S(2)}) async-start(f32[8,1,132096]{2,1,0:T(1,128)} %reshape.977), calls=%async_computation.3 | async-start | bytes 8454144 | tf_op jit(solution)/shard_map/all_to_all | solution.py:154
  815.1 12.6 %slice-start.2 = ((s8[6291456]{0:T(1024)(128)(4,1)}), s8[4194304]{0:T(1024)(128)(4,1)S(1)}, s32[]{:S(2)}) async-start(s8[6291456]{0:T(1024)(128)(4,1)} %bitcast.356), calls=%async_computation.6 | async-start | bytes 8388608
  815.1 12.6 %slice-start.3 = ((s8[6291456]{0:T(1024)(128)(4,1)}), s8[2097152]{0:T(1024)(128)(4,1)S(1)}, s32[]{:S(2)}) async-start(s8[6291456]{0:T(1024)(128)(4,1)} %bitcast.356), calls=%async_computation.7 | async-start | bytes 4194304
where the time goes:
time: 859 us; the launch traced here: 851 us
  matrix products  308 us (36%)
  local copies, waits for them, and re-layouts  198 us (23%)
  blocking collectives  154 us (18%)
  waiting for transfers between devices  141 us (16%)
  other arithmetic  39 us (5%)
  starting transfers between devices  9.87 us (1%)
    all_to_all x1, blocking collectives, local(): lax.all_to_all(first_send(spectrum, narrow_size), 'narrow', split_axis=0,...  102 us
    dot_general x8, matrix products, complex_product(): jnp.einsum(pattern, left_real, table_real, precision=highest)  96.5 us
    all_to_all x1, waiting for transfers between devices, local(): lax.all_to_all(outgoing, 'narrow', split_axis=0, concat_axis=1, tiled=True)  94.2 us
    dot_general x7, matrix products, complex_product(): jnp.einsum(pattern, left_real, table_imag, precision=highest)  76.1 us
    dot_general x8, matrix products, complex_product(): jnp.einsum(pattern, left_imag, table_imag, precision=highest)  74.8 us
    dot_general x7, matrix products, complex_product(): jnp.einsum(pattern, left_imag, table_real, precision=highest)  60.6 us
    all_to_all x1, blocking collectives, local(): lax.all_to_all(first_return(solved, narrow_size, wide_size, row_count), '...  52 us
    all_to_all x1, waiting for transfers between devices, local(): lax.all_to_all(outgoing, 'wide', split_axis=0, concat_axis=1, tiled=True)  47 us
  transfers between devices with their start and end apart: 2, of which 2 were waited for; matrix products, arithmetic and copies ran while one was open for 0% of the time, Pallas kernels for 0%

commit v1 on v0

--- a/solution.py
+++ b/solution.py
@@ -2,7 +2,10 @@
 
 import jax
 import jax.numpy as jnp
+import numpy as np
 from jax import lax
+from jax.experimental import pallas as pl
+from jax.experimental.pallas import tpu as pltpu
 from jax.sharding import PartitionSpec as P
 
 radix_split = 64
@@ -114,7 +117,7 @@
     return shaped.transpose(1, 2, 0, 3).reshape(groups, rows, -1)
 
 
-def local(velocity, plane_wavenumber):
+def local_generic(velocity, plane_wavenumber):
     components, plane_count, row_count, x_length = velocity.shape
     wide_size = lax.axis_size("wide")
     narrow_size = lax.axis_size("narrow")
@@ -162,6 +165,466 @@
     return out_real / x_length
 
 
+radix = 16
+lane = 128
+tile = 8
+axes = ("wide", "narrow")
+
+
+def split_parts(values):
+    high = values.astype(jnp.bfloat16)
+    low = (values - high.astype(jnp.float32)).astype(jnp.bfloat16)
+    return high, low
+
+
+def split_table(values):
+    values = values.astype(np.float32)
+    high = values.astype(jnp.bfloat16)
+    low = (values - high.astype(np.float32)).astype(jnp.bfloat16)
+    return high, low
+
+
+def turns(product, period):
+    angle = 2.0 * np.pi * (np.asarray(product) % period) / period
+    return np.cos(angle), np.sin(angle)
+
+
+def twist_table(inner):
+    return turns(np.arange(radix)[:, None] * np.arange(inner)[None, :], radix * inner)
+
+
+def line_slots(per_device):
+    main = per_device // tile * tile
+    half = tile // 2
+    slots = [(line, line, 0) for line in range(main)]
+    slots += [(main + line, line, 1) for line in range(main)]
+    for extra in range(per_device - main):
+        slots.append((2 * main + extra, main + extra, 0))
+        slots.append((2 * main + half + extra, main + extra, 1))
+    return slots
+
+
+def row_table(inner, per_device, shares, block):
+    rows = np.zeros((2 * shares * block, 2 * inner))
+    points = np.arange(inner)
+    for share in range(shares):
+        for row, line, part in line_slots(per_device):
+            q = share * per_device + line
+            cos, sin = turns(q * points, inner)
+            rows[share * block + row] = np.concatenate([-sin, cos] if part else [cos, sin])
+            cos, sin = turns((q + 1) * points, inner)
+            rows[(shares + share) * block + row] = np.concatenate([-sin, -cos] if part else [cos, -sin])
+    return rows
+
+
+def square_table(inner):
+    cos, sin = turns(np.arange(inner)[:, None] * np.arange(inner)[None, :], inner)
+    return np.block([[cos, -sin], [sin, cos]])
+
+
+def scaled(value, cos, sin):
+    real, imag = value
+    if abs(sin) < 1e-12:
+        return (real, imag) if cos > 0 else (-real, -imag)
+    if abs(cos) < 1e-12:
+        return (-imag, real) if sin > 0 else (imag, -real)
+    if abs(abs(cos) - abs(sin)) < 1e-12:
+        size = abs(cos)
+        a, b = (1.0 if cos > 0 else -1.0), (1.0 if sin > 0 else -1.0)
+        first = (real if a > 0 else -real) + (-imag if b > 0 else imag)
+        second = (real if b > 0 else -real) + (imag if a > 0 else -imag)
+        return first * size, second * size
+    return real * cos - imag * sin, real * sin + imag * cos
+
+
+def unit(step, size, direction):
+    angle = direction * 2.0 * math.pi * step / size
+    return math.cos(angle), math.sin(angle)
+
+
+def complex_fft(values, direction):
+    size = len(values)
+    if size == 1:
+        return values
+    even = complex_fft(values[0::2], direction)
+    odd = complex_fft(values[1::2], direction)
+    first, second = [], []
+    for k in range(size // 2):
+        real, imag = scaled(odd[k], *unit(k, size, direction))
+        first.append((even[k][0] + real, even[k][1] + imag))
+        second.append((even[k][0] - real, even[k][1] - imag))
+    return first + second
+
+
+def real_fft(values):
+    size = len(values)
+    if size == 2:
+        return [(values[0] + values[1], None), (values[0] - values[1], None)]
+    even = real_fft(values[0::2])
+    odd = real_fft(values[1::2])
+    quarter = size // 4
+    out = [None] * (size // 2 + 1)
+    out[0] = (even[0][0] + odd[0][0], None)
+    out[size // 2] = (even[0][0] - odd[0][0], None)
+    for k in range(1, quarter):
+        real, imag = scaled(odd[k], *unit(k, size, -1.0))
+        out[k] = (even[k][0] + real, even[k][1] + imag)
+        out[size // 2 - k] = (even[k][0] - real, imag - even[k][1])
+    out[quarter] = (even[quarter][0], -odd[quarter][0])
+    return out
+
+
+def real_sum(values):
+    count = len(values) - 1
+    size = 2 * count
+    if size == 2:
+        return [values[0][0] + values[1][0], values[0][0] - values[1][0]]
+    half = count // 2
+    even = [(values[0][0] + values[count][0], None)]
+    odd = [(values[0][0] - values[count][0], None)]
+    for s in range(1, half):
+        near, far = values[s], values[count - s]
+        even.append((near[0] + far[0], near[1] - far[1]))
+        odd.append(scaled((near[0] - far[0], near[1] + far[1]), *unit(s, size, 1.0)))
+    even.append((values[half][0], None))
+    odd.append((-values[half][1], None))
+    even_out, odd_out = real_sum(even), real_sum(odd)
+    out = []
+    for m in range(count):
+        out += [even_out[m], odd_out[m]]
+    return out
+
+
+def three_products(left, right, dims):
+    left_high, left_low = left
+    right_high, right_low = right
+
+    def one(a, b):
+        return lax.dot_general(a, b, (dims, ((), ())), preferred_element_type=jnp.float32)
+
+    return one(left_high, right_high) + one(left_low, right_high) + one(left_high, right_low)
+
+
+def slot_order():
+    return [0, radix // 2] + list(range(1, radix // 2))
+
+
+def rows_forward(x_ref, high_ref, low_ref, cos_ref, sin_ref, out_ref, th_ref, tl_ref, *, shares, block):
+    rows, length = x_ref.shape[2:]
+    inner = length // radix
+    order = slot_order()
+    chunk = 2 * tile
+
+    def vector_stage(step, carry):
+        start = pl.multiple_of(step * chunk, chunk)
+        for column in range(0, inner, lane):
+            parts = [
+                x_ref[0, 0, pl.ds(start, chunk), a * inner + column : a * inner + column + lane]
+                for a in range(radix)
+            ]
+            spectrum = real_fft(parts)
+            for slot, s in enumerate(order):
+                real, imag = spectrum[s]
+                if s:
+                    cos = cos_ref[s : s + 1, column : column + lane]
+                    sin = sin_ref[s : s + 1, column : column + lane]
+                    if imag is None:
+                        real, imag = real * cos, -(real * sin)
+                    else:
+                        real, imag = real * cos + imag * sin, imag * cos - real * sin
+                else:
+                    imag = jnp.zeros_like(real)
+                where = pl.ds(pl.multiple_of(slot * rows + start, chunk), chunk)
+                for offset, part in ((0, real), (inner, imag)):
+                    high, low = split_parts(part)
+                    th_ref[where, offset + column : offset + column + lane] = high
+                    tl_ref[where, offset + column : offset + column + lane] = low
+        return carry
+
+    lax.fori_loop(0, rows // chunk, vector_stage, 0)
+    nt = ((1,), (1,))
+    single = shares * block
+    slot = 0
+    while slot < len(order):
+        count = min(2, len(order) - slot)
+        height = single if slot == 0 else 2 * single
+        where = slice(slot * rows, (slot + count) * rows)
+        result = three_products(
+            (high_ref[:height], low_ref[:height]), (th_ref[where], tl_ref[where]), nt
+        )
+        for index in range(count):
+            s = order[slot + index]
+            columns = result[:, index * rows : (index + 1) * rows]
+            for share in range(shares):
+                out_ref[s * shares + share] = columns[share * block : (share + 1) * block]
+                if slot:
+                    out_ref[(radix - s) * shares + share] = columns[
+                        single + share * block : single + (share + 1) * block
+                    ]
+        slot += count
+
+
+def rows_back(in_ref, high_ref, low_ref, cos_ref, sin_ref, out_ref, g_ref, *, shares, block):
+    rows, length = out_ref.shape[2:]
+    inner = length // radix
+    order = slot_order()
+    depth = high_ref.shape[0]
+    for slot, s in enumerate(order):
+        blocks = [in_ref[s * shares + share] for share in range(shares)]
+        if slot > 1:
+            blocks += [in_ref[(radix - s) * shares + share] for share in range(shares)]
+        used = len(blocks) * block
+        wide = -(-used // lane) * lane
+        if wide > used:
+            blocks.append(jnp.zeros((wide - used, rows), jnp.float32))
+        turned = jnp.transpose(jnp.concatenate(blocks, axis=0))
+        keep = slice(0, wide)
+        g_ref[slot * rows : (slot + 1) * rows] = three_products(
+            split_parts(turned), (high_ref[keep], low_ref[keep]), ((1,), (0,))
+        )
+    chunk = tile
+
+    def vector_stage(step, carry):
+        start = pl.multiple_of(step * chunk, chunk)
+        for column in range(0, inner, lane):
+            values = [None] * len(order)
+            for slot, s in enumerate(order):
+                where = pl.ds(pl.multiple_of(slot * rows + start, chunk), chunk)
+                real = g_ref[where, column : column + lane]
+                if s:
+                    imag = g_ref[where, inner + column : inner + column + lane]
+                    cos = cos_ref[s : s + 1, column : column + lane]
+                    sin = sin_ref[s : s + 1, column : column + lane]
+                    if 2 * s == radix:
+                        real, imag = real * cos - imag * sin, None
+                    else:
+                        real, imag = real * cos - imag * sin, real * sin + imag * cos
+                else:
+                    imag = None
+                values[s] = (real, imag)
+            for a, out in enumerate(real_sum(values)):
+                out_ref[0, 0, pl.ds(start, chunk), a * inner + column : a * inner + column + lane] = out
+        return carry
+
+    lax.fori_loop(0, rows // chunk, vector_stage, 0)
+
+
+def lines_middle(
+    index_ref, wave_ref, in_ref, high_ref, low_ref, cos_ref, sin_ref, out_ref, th_ref, tl_ref, x_ref,
+    *, components, shares, block, per_device, keep_x, length_x
+):
+    rows = in_ref.shape[2]
+    inner = shares * rows
+    length_y = radix * inner
+    main = per_device // tile * tile
+    chunk = 2 * tile
+    padded = -(-(main + tile) // chunk) * chunk
+    group = radix * padded
+    half = tile // 2
+
+    def read(c, source, start):
+        real, imag = [], []
+        for row in range(start, start + chunk, tile):
+            if row < main:
+                real.append(in_ref[source, pl.ds(c * block + row, tile), :])
+                imag.append(in_ref[source, pl.ds(c * block + main + row, tile), :])
+            elif row == main:
+                last = in_ref[source, pl.ds(c * block + 2 * main, tile), :]
+                real.append(last)
+                imag.append(pltpu.roll(last, half, 0))
+            else:
+                real.append(jnp.zeros((tile, rows), jnp.float32))
+                imag.append(jnp.zeros((tile, rows), jnp.float32))
+        return jnp.concatenate(real, axis=0), jnp.concatenate(imag, axis=0)
+
+    def write(c, target, start, real, imag):
+        for position, row in enumerate(range(start, start + chunk, tile)):
+            a = real[position * tile : (position + 1) * tile]
+            b = imag[position * tile : (position + 1) * tile]
+            if row < main:
+                out_ref[target, pl.ds(c * block + row, tile), :] = a
+                out_ref[target, pl.ds(c * block + main + row, tile), :] = b
+            elif row == main:
+                index = lax.broadcasted_iota(jnp.int32, (tile, rows), 0)
+                out_ref[target, pl.ds(c * block + 2 * main, tile), :] = jnp.where(
+                    index < half, a, pltpu.roll(b, half, 0)
+                )
+
+    def forward(c, carry):
+        for start in range(0, padded, chunk):
+            for share in range(shares):
+                column = share * rows
+                values = [read(c, a * shares + share, start) for a in range(radix)]
+                for s, (real, imag) in enumerate(complex_fft(values, -1.0)):
+                    if s:
+                        cos = cos_ref[s : s + 1, column : column + rows]
+                        sin = sin_ref[s : s + 1, column : column + rows]
+                        real, imag = real * cos + imag * sin, imag * cos - real * sin
+                    where = slice(s * padded + start, s * padded + start + chunk)
+                    for offset, part in ((0, real), (inner, imag)):
+                        high, low = split_parts(part)
+                        th_ref[c, where, offset + column : offset + column + rows] = high
+                        tl_ref[c, where, offset + column : offset + column + rows] = low
+        return carry
+
+    lax.fori_loop(0, components, forward, 0)
+
+    def products(dims):
+        def run(step, carry):
+            c = step // 2
+            where = pl.ds(pl.multiple_of((step % 2) * (group // 2), chunk), group // 2)
+            x_ref[c, where, :] = three_products(
+                (th_ref[c, where, :], tl_ref[c, where, :]), (high_ref[...], low_ref[...]), dims
+            )
+            return carry
+
+        lax.fori_loop(0, 2 * components, run, 0)
+
+    products(((1,), (0,)))
+
+    share_of = index_ref[0] % shares
+    offset_of = index_ref[0] // shares
+    wave_z = wave_ref[0]
+    scale = 1.0 / (length_x * length_y)
+
+    def middle(s, carry):
+        for start in range(0, padded, chunk):
+            line = lax.broadcasted_iota(jnp.int32, (chunk, inner), 0) + start
+            line_x = (share_of * per_device + line) * radix + offset_of
+            index_y = lax.broadcasted_iota(jnp.int32, (chunk, inner), 1) * radix + s
+            signed_y = jnp.where(index_y <= length_y // 2, index_y, index_y - length_y)
+            kept = (line < per_device) & (line_x < keep_x) & (jnp.abs(signed_y) <= length_y // 3)
+            weight = jnp.where(line_x == 0, scale, 2.0 * scale)
+            factor = jnp.where(kept, weight, 0.0)
+            wave_x = line_x.astype(jnp.float32)
+            wave_y = signed_y.astype(jnp.float32)
+            waves = (wave_x, wave_y, wave_z)
+            inverse = factor / (wave_x * wave_x + wave_y * wave_y + wave_z * wave_z)
+            where = pl.ds(pl.multiple_of(s * padded + start, chunk), chunk)
+            for offset in (0, inner):
+                columns = slice(offset, offset + inner)
+                values = [x_ref[c, where, columns] for c in range(components)]
+                divergence = (
+                    wave_x * values[0] + wave_y * values[1] + wave_z * values[2]
+                ) * inverse
+                for c in range(components):
+                    high, low = split_parts(factor * values[c] - waves[c] * divergence)
+                    th_ref[c, where, columns] = high
+                    tl_ref[c, where, columns] = low
+        return carry
+
+    lax.fori_loop(0, radix, middle, 0)
+    products(((1,), (1,)))
+
+    def backward(c, carry):
+        for start in range(0, padded, chunk):
+            for share in range(shares):
+                column = share * rows
+                values = []
+                for s in range(radix):
+                    where = slice(s * padded + start, s * padded + start + chunk)
+                    real = x_ref[c, where, column : column + rows]
+                    imag = x_ref[c, where, inner + column : inner + column + rows]
+                    if s:
+                        cos = cos_ref[s : s + 1, column : column + rows]
+                        sin = sin_ref[s : s + 1, column : column + rows]
+                        real, imag = real * cos - imag * sin, real * sin + imag * cos
+                    values.append((real, imag))
+                for a, (real, imag) in enumerate(complex_fft(values, 1.0)):
+                    write(c, a * shares + share, start, real, imag)
+        return carry
+
+    lax.fori_loop(0, components, backward, 0)
+
+
+def whole(shape):
+    return pl.BlockSpec(shape, lambda *_: (0,) * len(shape))
+
+
+def local_fast(velocity, plane_wavenumber):
+    components, _, rows, length_x = velocity.shape
+    devices = lax.axis_size("wide") * lax.axis_size("narrow")
+    keep_x = length_x // 3 + 1
+    inner = length_x // radix
+    shares = devices // radix
+    per_device = -(-keep_x // (radix * shares))
+    main = per_device // tile * tile
+    block = 2 * main + tile
+    padded = -(-(main + tile) // (2 * tile)) * 2 * tile
+    table = row_table(inner, per_device, shares, block)
+    table = np.pad(table, ((0, -len(table) % lane), (0, 0)))
+    row_high, row_low = (jnp.asarray(t) for t in split_table(table))
+    line_inner = shares * rows
+    line_high, line_low = (jnp.asarray(t) for t in split_table(square_table(line_inner)))
+    row_cos, row_sin = (jnp.asarray(t, jnp.float32) for t in twist_table(inner))
+    line_cos, line_sin = (jnp.asarray(t, jnp.float32) for t in twist_table(line_inner))
+    limits = pltpu.CompilerParams(vmem_limit_bytes=56 * 1024 * 1024)
+    row_tables = (row_high, row_low, row_cos, row_sin)
+    row_specs = [whole(t.shape) for t in row_tables]
+    slots = radix // 2 + 1
+    field_spec = pl.BlockSpec((1, 1, rows, length_x), lambda c: (c, 0, 0, 0))
+    line_spec = pl.BlockSpec((devices, block, rows), lambda c: (0, c, 0))
+    line_shape = jax.ShapeDtypeStruct((devices, components * block, rows), jnp.float32)
+    spectrum = pl.pallas_call(
+        lambda *refs: rows_forward(*refs, shares=shares, block=block),
+        grid=(components,),
+        in_specs=[field_spec] + row_specs,
+        out_specs=line_spec,
+        out_shape=line_shape,
+        scratch_shapes=[pltpu.VMEM((slots * rows, 2 * inner), jnp.bfloat16)] * 2,
+        compiler_params=limits,
+        name="rows_forward",
+    )(velocity, *row_tables)
+    lines = lax.all_to_all(spectrum, axes, split_axis=0, concat_axis=0, tiled=True)
+    index = lax.axis_index(axes).astype(jnp.int32).reshape(1)
+    line_tables = (line_high, line_low, line_cos, line_sin)
+    scalar = pl.BlockSpec(memory_space=pltpu.SMEM)
+    solved = pl.pallas_call(
+        lambda *refs: lines_middle(
+            *refs, components=components, shares=shares, block=block, per_device=per_device,
+            keep_x=keep_x, length_x=length_x,
+        ),
+        grid=(1,),
+        in_specs=[scalar, scalar, whole(line_shape.shape)] + [whole(t.shape) for t in line_tables],
+        out_specs=whole(line_shape.shape),
+        out_shape=line_shape,
+        scratch_shapes=[pltpu.VMEM((components, radix * padded, 2 * line_inner), jnp.bfloat16)] * 2
+        + [pltpu.VMEM((components, radix * padded, 2 * line_inner), jnp.float32)],
+        compiler_params=limits,
+        name="lines_middle",
+    )(index, plane_wavenumber, lines, *line_tables)
+    returned = lax.all_to_all(solved, axes, split_axis=0, concat_axis=0, tiled=True)
+    return pl.pallas_call(
+        lambda *refs: rows_back(*refs, shares=shares, block=block),
+        grid=(components,),
+        in_specs=[line_spec] + row_specs,
+        out_specs=field_spec,
+        out_shape=jax.ShapeDtypeStruct(velocity.shape, jnp.float32),
+        scratch_shapes=[pltpu.VMEM((slots * rows, 2 * inner), jnp.float32)],
+        compiler_params=limits,
+        name="rows_back",
+    )(returned, *row_tables)
+
+
+def local(velocity, plane_wavenumber):
+    components, planes, rows, length_x = velocity.shape
+    devices = lax.axis_size("wide") * lax.axis_size("narrow")
+    keep_x = length_x // 3 + 1
+    fits = (
+        components == 3
+        and planes == 1
+        and rows == lane
+        and length_x % (radix * lane) == 0
+        and devices % radix == 0
+        and -(-keep_x // devices) == -(-(-(-keep_x // radix)) // (devices // radix))
+        and -(-keep_x // devices) % tile <= tile // 2
+        and (rows * devices) // 3 < rows * devices // 2
+    )
+    if fits:
+        return local_fast(velocity, plane_wavenumber)
+    return local_generic(velocity, plane_wavenumber)
+
+
 def solution(mesh):
     placed = (P(None, None, ("wide", "narrow"), None), P())
     return jax.shard_map(

time: 859 us -> 248 us (0.29)
  matrix products: 308 us -> 0 us
  local copies, waits for them, and re-layouts: 198 us -> 0 us
  blocking collectives: 154 us -> 101 us
  waiting for transfers between devices: 141 us -> 98 us
  Pallas kernels: 0 us -> 40.6 us
  other arithmetic: 39 us -> 0 us
    dot_general x30 -> x0, matrix products: 308 us -> none  [the longest x8 96.5 us: complex_product(): jnp.einsum(pattern, left_real, table_real, precision=highest)]
    reshape x6 -> x0, local copies, waits for them, and re-layouts: 86.5 us -> none  [the longest x1 26.8 us: second_send(): shaped = received.reshape(first_size, groups, rows, second_size, per_device)]
    all_to_all x2 -> x1, blocking collectives: 154 us -> 101 us  [local_fast(): lax.all_to_all(solved, axes, split_axis=0, concat_axis=0, tiled=True)]
    all_to_all x2 -> x1, waiting for transfers between devices: 141 us -> 98 us  [local_fast(): lax.all_to_all(spectrum, axes, split_axis=0, concat_axis=0, tiled=True)]
    pallas_call x0 -> x3, Pallas kernels: none -> 40.6 us  [the longest x1 19.7 us: local_fast(): pl.pallas_call(lambda *refs: lines_middle(*refs, components=components, s...]
    another operation x9 -> x0, local copies, waits for them, and re-layouts: 33.3 us -> none
    all_to_all x2 -> x0, other arithmetic: 26.6 us -> none  [the longest x1 13.4 us: local(): lax.all_to_all(first_send(spectrum, narrow_size), 'narrow', split_axis=0,...]
    transpose x4 -> x0, local copies, waits for them, and re-layouts: 23.8 us -> none  [the longest x1 9.21 us: second_send(): return shaped.transpose(3, 1, 4, 0, 2).reshape(second_size, 1, -1)]
  transfers between devices with their start and end apart: 2 -> 1, of which waited for: 2 -> 1; matrix products, arithmetic and copies ran while one was open for 0% -> 0% of each run, Pallas kernels for 0% -> 0%
where the time goes in v1:
time: 248 us
  blocking collectives  101 us (41%)
  waiting for transfers between devices  98 us (40%)
  Pallas kernels  40.6 us (16%)
  starting transfers between devices  7.44 us (3%)
    all_to_all x1, blocking collectives, local_fast(): lax.all_to_all(solved, axes, split_axis=0, concat_axis=0, tiled=True)  101 us
    all_to_all x1, waiting for transfers between devices, local_fast(): lax.all_to_all(spectrum, axes, split_axis=0, concat_axis=0, tiled=True)  98 us
    pallas_call x1, Pallas kernels, local_fast(): pl.pallas_call(lambda *refs: lines_middle(*refs, components=components, s...  19.7 us
    pallas_call x1, Pallas kernels, local_fast(): pl.pallas_call(lambda *refs: rows_back(*refs, shares=shares, block=block)...  10.5 us
    pallas_call x1, Pallas kernels, local_fast(): pl.pallas_call(lambda *refs: rows_forward(*refs, shares=shares, block=blo...  10.4 us
    all_to_all x1, starting transfers between devices, local_fast(): lax.all_to_all(spectrum, axes, split_axis=0, concat_axis=0, tiled=True)  7.44 us
  transfers between devices with their start and end apart: 1, of which 1 were waited for; matrix products, arithmetic and copies ran while one was open for 0% of the time, Pallas kernels for 0%

profile of v1, /device:TPU:0, one launch (start us, length us, event | category | flops | bytes accessed | tf_op | source)
XLA Modules:
  0.0 248.0 jit_solution(17875351011136426926)
XLA Ops:
  0.0 10.4 %rows_forward.1 = f32[32,264,128]{2,1,0:T(8,128)} custom-call(f32[3,1,128,4096]{3,2,1,0:T(8,128)} %refs_0_.1, bf16[384,512]{1,0:T(8,128)(2,1)} %constant.22.clone.refs_1_, bf16[384,512]{1,0:T(8,128)(2,1)} %constant.23.clone.refs_2_, f32[16,256]{1,0:T(8,128)} %constant.26.clone.refs_3_.refs_5_, f32[16,256]{1,0:T(8,128)} %constant.27.clone.refs_4_.refs_6_), custom_call_target="tpu_custom_call" | custom-call | tf_op jit(solution)/shard_map/rows_forward/pallas_call | solution.py:568
  10.4 7.4 %all-to-all-start = ((f32[32,264,128]{2,1,0:T(8,128)}), f32[32,264,128]{2,1,0:T(8,128)}, u32[]{:S(2)}, u32[]{:S(2)}) async-start(f32[32,264,128]{2,1,0:T(8,128)} %rows_forward.1), calls=%async_computation | async-start | bytes 8650752 | tf_op jit(solution)/shard_map/all_to_all | solution.py:578
  18.5 98.0 %all-to-all-done.refs_2_ = f32[32,264,128]{2,1,0:T(8,128)} async-done(((f32[32,264,128]{2,1,0:T(8,128)}), f32[32,264,128]{2,1,0:T(8,128)}, u32[]{:S(2)}, u32[]{:S(2)}) %all-to-all-start) | async-done | bytes 4325408 | tf_op jit(solution)/shard_map/all_to_all | solution.py:578
  116.5 19.7 %lines_middle.1 = f32[32,264,128]{2,1,0:T(8,128)} custom-call(s32[1]{0:T(128)} %bitcast.refs_0_, f32[1]{0:T(128)S(6)} %copy.11.refs_1_, f32[32,264,128]{2,1,0:T(8,128)} %all-to-all-done.refs_2_, bf16[512,512]{1,0:T(8,128)(2,1)} %constant.24.clone.refs_3_, bf16[512,512]{1,0:T(8,128)(2,1)} %constant.25.clone.refs_4_, ...), custom_call_target="tpu_custom_call" | custom-call | tf_op jit(solution)/shard_map/lines_middle/pallas_call | solution.py:582
  136.2 101.2 %all_to_all.10.refs_0_ = f32[32,264,128]{2,1,0:T(8,128)} all-to-all(f32[32,264,128]{2,1,0:T(8,128)} %lines_middle.1), channel_id=1, replica_groups=mesh['wide'=4,'narrow'=8] {'wide','narrow'}, dimensions={0} | all-to-all | bytes 8650752 | tf_op jit(solution)/shard_map/all_to_all | solution.py:596
  237.5 10.5 %rows_back.1 = f32[3,1,128,4096]{3,2,1,0:T(8,128)} custom-call(f32[32,264,128]{2,1,0:T(8,128)} %all_to_all.10.refs_0_, bf16[384,512]{1,0:T(8,128)(2,1)} %constant.22.clone.refs_1_, bf16[384,512]{1,0:T(8,128)(2,1)} %constant.23.clone.refs_2_, f32[16,256]{1,0:T(8,128)} %constant.26.clone.refs_3_.refs_5_, f32[16,256]{1,0:T(8,128)} %constant.27.clone.refs_4_.refs_6_), custom_call_target="tpu_custom_call" | custom-call | tf_op jit(solution)/shard_map/rows_back/pallas_call | solution.py:597
Async XLA Ops:
  10.4 106.1 %all-to-all-start = ((f32[32,264,128]{2,1,0:T(8,128)}), f32[32,264,128]{2,1,0:T(8,128)}, u32[]{:S(2)}, u32[]{:S(2)}) async-start(f32[32,264,128]{2,1,0:T(8,128)} %rows_forward.1), calls=%async_computation | async-start | bytes 8650752 | tf_op jit(solution)/shard_map/all_to_all | solution.py:578

commit v2 on v1

--- a/solution.py
+++ b/solution.py
@@ -1,3 +1,4 @@
+import functools
 import math
 
 import jax
@@ -7,6 +8,7 @@
 from jax.experimental import pallas as pl
 from jax.experimental.pallas import tpu as pltpu
 from jax.sharding import PartitionSpec as P
+
 
 radix_split = 64
 highest = lax.Precision.HIGHEST
@@ -161,7 +163,7 @@
     widen = ((0, 0), (0, 0), (0, 0), (0, x_length - keep_x))
     back_real = jnp.pad(columns[:, 0] * weights, widen)
     back_imag = jnp.pad(columns[:, 1] * weights, widen)
-    out_real, out_imag = transform(back_real, back_imag, 1.0)
+    out_real, _ = transform(back_real, back_imag, 1.0)
     return out_real / x_length
 
 
@@ -193,14 +195,24 @@
     return turns(np.arange(radix)[:, None] * np.arange(inner)[None, :], radix * inner)
 
 
+def line_chunks(per_device):
+    first = per_device // (4 * tile) * (2 * tile)
+    last = per_device - first
+    main = last // tile * tile
+    return ((0, first, first, 2 * first), (first, last, main, 2 * main + tile))
+
+
 def line_slots(per_device):
-    main = per_device // tile * tile
     half = tile // 2
-    slots = [(line, line, 0) for line in range(main)]
-    slots += [(main + line, line, 1) for line in range(main)]
-    for extra in range(per_device - main):
-        slots.append((2 * main + extra, main + extra, 0))
-        slots.append((2 * main + half + extra, main + extra, 1))
+    base = 0
+    slots = []
+    for start, lines, main, height in line_chunks(per_device):
+        slots += [(base + line, start + line, 0) for line in range(main)]
+        slots += [(base + main + line, start + line, 1) for line in range(main)]
+        for extra in range(lines - main):
+            slots.append((base + 2 * main + extra, start + main + extra, 0))
+            slots.append((base + 2 * main + half + extra, start + main + extra, 1))
+        base += height
     return slots
 
 
@@ -309,7 +321,12 @@
     return [0, radix // 2] + list(range(1, radix // 2))
 
 
-def rows_forward(x_ref, high_ref, low_ref, cos_ref, sin_ref, out_ref, th_ref, tl_ref, *, shares, block):
+def rows_forward(
+    index_ref, x_ref, high_ref, low_ref, cos_ref, sin_ref, near_ref, *refs, shares, block
+):
+    far_refs = refs[:-3]
+    th_ref, tl_ref, box_ref = refs[-3:]
+    split = near_ref.shape[1]
     rows, length = x_ref.shape[2:]
     inner = length // radix
     order = slot_order()
@@ -356,24 +373,33 @@
             s = order[slot + index]
             columns = result[:, index * rows : (index + 1) * rows]
             for share in range(shares):
-                out_ref[s * shares + share] = columns[share * block : (share + 1) * block]
-                if slot:
-                    out_ref[(radix - s) * shares + share] = columns[
-                        single + share * block : single + (share + 1) * block
-                    ]
+                targets = [(s, share)] + ([(radix - s, shares + share)] if slot else [])
+                for residue, position in targets:
+                    piece = columns[position * block : (position + 1) * block]
+                    near_ref[residue * shares + share] = piece[:split]
+                    box_ref[residue * shares + share] = piece[split:]
         slot += count
-
-
-def rows_back(in_ref, high_ref, low_ref, cos_ref, sin_ref, out_ref, g_ref, *, shares, block):
+    height = block - split
+    where = pl.ds(pl.program_id(0) * height, height)
+    for k, far_ref in enumerate(far_refs):
+        far_ref[where, :] = box_ref[index_ref[0] ^ k]
+
+
+def rows_back(index_ref, near_ref, high_ref, low_ref, cos_ref, sin_ref, *refs, shares, block):
+    out_ref, g_ref, far_ref = refs[-3:]
+    devices, height = far_ref.shape[:2]
+    place = pl.ds(pl.program_id(0) * height, height)
+    for k in range(devices):
+        far_ref[index_ref[0] ^ k] = refs[k][place, :]
     rows, length = out_ref.shape[2:]
     inner = length // radix
     order = slot_order()
-    depth = high_ref.shape[0]
     for slot, s in enumerate(order):
-        blocks = [in_ref[s * shares + share] for share in range(shares)]
-        if slot > 1:
-            blocks += [in_ref[(radix - s) * shares + share] for share in range(shares)]
-        used = len(blocks) * block
+        blocks = []
+        for residue in [s] if slot < 2 else [s, radix - s]:
+            for share in range(shares):
+                blocks += [near_ref[residue * shares + share], far_ref[residue * shares + share]]
+        used = len(blocks) // 2 * block
         wide = -(-used // lane) * lane
         if wide > used:
             blocks.append(jnp.zeros((wide - used, rows), jnp.float32))
@@ -410,19 +436,23 @@
 
 
 def lines_middle(
-    index_ref, wave_ref, in_ref, high_ref, low_ref, cos_ref, sin_ref, out_ref, th_ref, tl_ref, x_ref,
-    *, components, shares, block, per_device, keep_x, length_x
+    index_ref, wave_ref, *refs, counts, targets, shares, chunk_shape, per_device, keep_x, length_x
 ):
-    rows = in_ref.shape[2]
+    in_refs = refs[: len(counts)]
+    high_ref, low_ref, cos_ref, sin_ref = refs[len(counts) : len(counts) + 4]
+    th_ref, tl_ref, x_ref = refs[-3:]
+    out_refs = refs[-3 - len(targets) : -3]
+    first, lines, main, block = chunk_shape
+    components = sum(counts)
+    rows = in_refs[0].shape[2]
     inner = shares * rows
     length_y = radix * inner
-    main = per_device // tile * tile
     chunk = 2 * tile
-    padded = -(-(main + tile) // chunk) * chunk
+    padded = -(-lines // chunk) * chunk
     group = radix * padded
     half = tile // 2
 
-    def read(c, source, start):
+    def read(in_ref, c, source, start):
         real, imag = [], []
         for row in range(start, start + chunk, tile):
             if row < main:
@@ -437,7 +467,7 @@
                 imag.append(jnp.zeros((tile, rows), jnp.float32))
         return jnp.concatenate(real, axis=0), jnp.concatenate(imag, axis=0)
 
-    def write(c, target, start, real, imag):
+    def write(out_ref, c, target, start, real, imag):
         for position, row in enumerate(range(start, start + chunk, tile)):
             a = real[position * tile : (position + 1) * tile]
             b = imag[position * tile : (position + 1) * tile]
@@ -450,11 +480,14 @@
                     index < half, a, pltpu.roll(b, half, 0)
                 )
 
-    def forward(c, carry):
+    def forward(in_ref, base, position, carry):
+        c = base + position
         for start in range(0, padded, chunk):
             for share in range(shares):
                 column = share * rows
-                values = [read(c, a * shares + share, start) for a in range(radix)]
+                values = [
+                    read(in_ref, position, a * shares + share, start) for a in range(radix)
+                ]
                 for s, (real, imag) in enumerate(complex_fft(values, -1.0)):
                     if s:
                         cos = cos_ref[s : s + 1, column : column + rows]
@@ -467,7 +500,10 @@
                         tl_ref[c, where, offset + column : offset + column + rows] = low
         return carry
 
-    lax.fori_loop(0, components, forward, 0)
+    base = 0
+    for in_ref, count in zip(in_refs, counts):
+        lax.fori_loop(0, count, functools.partial(forward, in_ref, base), 0)
+        base += count
 
     def products(dims):
         def run(step, carry):
@@ -490,10 +526,10 @@
     def middle(s, carry):
         for start in range(0, padded, chunk):
             line = lax.broadcasted_iota(jnp.int32, (chunk, inner), 0) + start
-            line_x = (share_of * per_device + line) * radix + offset_of
+            line_x = (share_of * per_device + first + line) * radix + offset_of
             index_y = lax.broadcasted_iota(jnp.int32, (chunk, inner), 1) * radix + s
             signed_y = jnp.where(index_y <= length_y // 2, index_y, index_y - length_y)
-            kept = (line < per_device) & (line_x < keep_x) & (jnp.abs(signed_y) <= length_y // 3)
+            kept = (line < lines) & (line_x < keep_x) & (jnp.abs(signed_y) <= length_y // 3)
             weight = jnp.where(line_x == 0, scale, 2.0 * scale)
             factor = jnp.where(kept, weight, 0.0)
             wave_x = line_x.astype(jnp.float32)
@@ -516,7 +552,8 @@
     lax.fori_loop(0, radix, middle, 0)
     products(((1,), (1,)))
 
-    def backward(c, carry):
+    def backward(out_ref, base, position, carry):
+        c = base + position
         for start in range(0, padded, chunk):
             for share in range(shares):
                 column = share * rows
@@ -531,14 +568,33 @@
                         real, imag = real * cos - imag * sin, real * sin + imag * cos
                     values.append((real, imag))
                 for a, (real, imag) in enumerate(complex_fft(values, 1.0)):
-                    write(c, a * shares + share, start, real, imag)
+                    write(out_ref, position, a * shares + share, start, real, imag)
         return carry
 
-    lax.fori_loop(0, components, backward, 0)
+    base = 0
+    for out_ref, count in zip(out_refs, targets):
+        lax.fori_loop(0, count, functools.partial(backward, out_ref, base), 0)
+        base += count
 
 
 def whole(shape):
     return pl.BlockSpec(shape, lambda *_: (0,) * len(shape))
+
+
+def token_of(in_ref, out_ref):
+    out_ref[...] = in_ref[0]
+
+
+def exchange(values):
+    return lax.all_to_all(values, axes, split_axis=0, concat_axis=0, tiled=True)
+
+
+def swap(blocks):
+    count = len(blocks)
+    moved = list(blocks)
+    for k in range(1, count):
+        moved[k] = lax.ppermute(blocks[k], axes, [(source, source ^ k) for source in range(count)])
+    return moved
 
 
 def local_fast(velocity, plane_wavenumber):
@@ -548,62 +604,119 @@
     inner = length_x // radix
     shares = devices // radix
     per_device = -(-keep_x // (radix * shares))
-    main = per_device // tile * tile
-    block = 2 * main + tile
-    padded = -(-(main + tile) // (2 * tile)) * 2 * tile
+    near, far = line_chunks(per_device)
+    block = near[3] + far[3]
     table = row_table(inner, per_device, shares, block)
     table = np.pad(table, ((0, -len(table) % lane), (0, 0)))
-    row_high, row_low = (jnp.asarray(t) for t in split_table(table))
     line_inner = shares * rows
-    line_high, line_low = (jnp.asarray(t) for t in split_table(square_table(line_inner)))
-    row_cos, row_sin = (jnp.asarray(t, jnp.float32) for t in twist_table(inner))
-    line_cos, line_sin = (jnp.asarray(t, jnp.float32) for t in twist_table(line_inner))
+    row_tables = [jnp.asarray(t) for t in split_table(table)]
+    row_tables += [jnp.asarray(t, jnp.float32) for t in twist_table(inner)]
+    line_tables = [jnp.asarray(t) for t in split_table(square_table(line_inner))]
+    line_tables += [jnp.asarray(t, jnp.float32) for t in twist_table(line_inner)]
     limits = pltpu.CompilerParams(vmem_limit_bytes=56 * 1024 * 1024)
-    row_tables = (row_high, row_low, row_cos, row_sin)
-    row_specs = [whole(t.shape) for t in row_tables]
     slots = radix // 2 + 1
-    field_spec = pl.BlockSpec((1, 1, rows, length_x), lambda c: (c, 0, 0, 0))
-    line_spec = pl.BlockSpec((devices, block, rows), lambda c: (0, c, 0))
-    line_shape = jax.ShapeDtypeStruct((devices, components * block, rows), jnp.float32)
-    spectrum = pl.pallas_call(
-        lambda *refs: rows_forward(*refs, shares=shares, block=block),
+    anywhere = pl.BlockSpec(memory_space=pl.ANY)
+    scalar = pl.BlockSpec(memory_space=pltpu.SMEM)
+    index = lax.axis_index(axes).astype(jnp.int32).reshape(1)
+
+    def shape(count, height):
+        return jax.ShapeDtypeStruct((devices, count * height, rows), jnp.float32)
+
+    def single(count):
+        return jax.ShapeDtypeStruct((count * far[3], rows), jnp.float32)
+
+    def box(count):
+        return pltpu.VMEM((devices, count * far[3], rows), jnp.float32)
+
+    def component(height):
+        return pl.BlockSpec((devices, height, rows), lambda c: (0, c, 0))
+
+    field = pl.BlockSpec((1, 1, rows, length_x), lambda c: (c, 0, 0, 0))
+
+    near_lines, *far_lines = pl.pallas_call(
+        functools.partial(rows_forward, shares=shares, block=block),
         grid=(components,),
-        in_specs=[field_spec] + row_specs,
-        out_specs=line_spec,
-        out_shape=line_shape,
-        scratch_shapes=[pltpu.VMEM((slots * rows, 2 * inner), jnp.bfloat16)] * 2,
+        in_specs=[scalar, field] + [whole(t.shape) for t in row_tables],
+        out_specs=[component(near[3])] + [whole(single(components).shape)] * devices,
+        out_shape=[shape(components, near[3])] + [single(components)] * devices,
+        scratch_shapes=[pltpu.VMEM((slots * rows, 2 * inner), jnp.bfloat16)] * 2 + [box(1)],
         compiler_params=limits,
         name="rows_forward",
-    )(velocity, *row_tables)
-    lines = lax.all_to_all(spectrum, axes, split_axis=0, concat_axis=0, tiled=True)
-    index = lax.axis_index(axes).astype(jnp.int32).reshape(1)
-    line_tables = (line_high, line_low, line_cos, line_sin)
-    scalar = pl.BlockSpec(memory_space=pltpu.SMEM)
-    solved = pl.pallas_call(
-        lambda *refs: lines_middle(
-            *refs, components=components, shares=shares, block=block, per_device=per_device,
-            keep_x=keep_x, length_x=length_x,
-        ),
+    )(index, velocity, *row_tables)
+
+    def middle(sources, targets, chunk_shape):
+        spread = len(sources) > 1
+        height = chunk_shape[3]
+        padded = -(-chunk_shape[1] // (2 * tile)) * 2 * tile
+        group = (components, radix * padded, 2 * line_inner)
+        outs = [shape(count, height) for count in targets]
+        if spread:
+            outs = outs[:-1] + [single(targets[-1])] * devices
+        place = 2 + len(sources) + len(line_tables)
+
+        def body(*refs):
+            index_ref, wave_ref = refs[:2]
+            from_refs, tables = refs[2 : 2 + len(sources)], refs[2 + len(sources) : place]
+            to_refs, scratch = refs[place : place + len(outs)], refs[place + len(outs) :]
+            spread_refs = to_refs[-devices:]
+            if spread:
+                in_box, out_box, *scratch = scratch
+                for k, ref in enumerate(from_refs):
+                    in_box[index_ref[0] ^ k] = ref[...]
+                from_refs, to_refs = [in_box], to_refs[:-devices] + (out_box,)
+            lines_middle(
+                index_ref, wave_ref, *from_refs, *tables, *to_refs, *scratch, counts=(components,),
+                targets=targets, shares=shares, chunk_shape=chunk_shape, per_device=per_device,
+                keep_x=keep_x, length_x=length_x,
+            )
+            if spread:
+                for k, ref in enumerate(spread_refs):
+                    ref[...] = out_box[index_ref[0] ^ k]
+
+        return pl.pallas_call(
+            body,
+            grid=(1,),
+            in_specs=[scalar, scalar]
+            + [whole(t.shape) for t in sources]
+            + [whole(t.shape) for t in line_tables],
+            out_specs=[whole(t.shape) for t in outs],
+            out_shape=outs,
+            scratch_shapes=([box(components), box(targets[-1])] if spread else [])
+            + [pltpu.VMEM(group, jnp.bfloat16)] * 2
+            + [pltpu.VMEM(group, jnp.float32)],
+            compiler_params=limits,
+        )(index, plane_wavenumber, *sources, *line_tables)
+
+    def back(near_lines, far_lines, token):
+        return pl.pallas_call(
+            functools.partial(rows_back, shares=shares, block=block),
+            grid=(components,),
+            in_specs=[scalar, component(near[3])]
+            + [whole(t.shape) for t in row_tables]
+            + [whole(single(components).shape)] * devices
+            + [anywhere],
+            out_specs=field,
+            out_shape=jax.ShapeDtypeStruct(velocity.shape, jnp.float32),
+            scratch_shapes=[pltpu.VMEM((slots * rows, 2 * inner), jnp.float32), box(1)],
+            compiler_params=limits,
+            name="rows_back",
+        )(index, near_lines, *row_tables, *far_lines, token)
+
+    near_lines = exchange(near_lines)
+    far_lines = swap(far_lines)
+    (near_lines,) = middle([near_lines], (components,), near)
+    near_lines = exchange(near_lines)
+    far_lines = middle(far_lines, (components,), far)
+    far_lines = swap(far_lines)
+    token = pl.pallas_call(
+        token_of,
         grid=(1,),
-        in_specs=[scalar, scalar, whole(line_shape.shape)] + [whole(t.shape) for t in line_tables],
-        out_specs=whole(line_shape.shape),
-        out_shape=line_shape,
-        scratch_shapes=[pltpu.VMEM((components, radix * padded, 2 * line_inner), jnp.bfloat16)] * 2
-        + [pltpu.VMEM((components, radix * padded, 2 * line_inner), jnp.float32)],
-        compiler_params=limits,
-        name="lines_middle",
-    )(index, plane_wavenumber, lines, *line_tables)
-    returned = lax.all_to_all(solved, axes, split_axis=0, concat_axis=0, tiled=True)
-    return pl.pallas_call(
-        lambda *refs: rows_back(*refs, shares=shares, block=block),
-        grid=(components,),
-        in_specs=[line_spec] + row_specs,
-        out_specs=field_spec,
-        out_shape=jax.ShapeDtypeStruct(velocity.shape, jnp.float32),
-        scratch_shapes=[pltpu.VMEM((slots * rows, 2 * inner), jnp.float32)],
-        compiler_params=limits,
-        name="rows_back",
-    )(returned, *row_tables)
+        in_specs=[pl.BlockSpec((1, tile, lane), lambda _: (0, 0, 0))],
+        out_specs=whole((tile, lane)),
+        out_shape=jax.ShapeDtypeStruct((tile, lane), jnp.float32),
+        name="near_token",
+    )(near_lines)
+    return back(near_lines, far_lines, token)
 
 
 def local(velocity, plane_wavenumber):
@@ -616,6 +729,7 @@
         and rows == lane
         and length_x % (radix * lane) == 0
         and devices % radix == 0
+        and devices & (devices - 1) == 0
         and -(-keep_x // devices) == -(-(-(-keep_x // radix)) // (devices // radix))
         and -(-keep_x // devices) % tile <= tile // 2
         and (rows * devices) // 3 < rows * devices // 2
@@ -627,6 +741,7 @@
 
 def solution(mesh):
     placed = (P(None, None, ("wide", "narrow"), None), P())
+
     return jax.shard_map(
         local,
         mesh=mesh,

time: 248 us -> 288 us (1.16)
  starting transfers between devices: 7.44 us -> 116 us
  blocking collectives: 101 us -> 0 us
  waiting for transfers between devices: 98 us -> 115 us
  Pallas kernels: 40.6 us -> 50.1 us
  local copies, waits for them, and re-layouts: 0 us -> 3.6 us
    ppermute x0 -> x62, starting transfers between devices: none -> 106 us  [swap(): lax.ppermute(blocks[k], axes, [(source, source ^ k) for source in range(c...]
    all_to_all x1 -> x0, blocking collectives: 101 us -> none  [local_fast(): lax.all_to_all(solved, axes, split_axis=0, concat_axis=0, tiled=True)]
    ppermute x0 -> x62, waiting for transfers between devices: none -> 76.4 us  [swap(): lax.ppermute(blocks[k], axes, [(source, source ^ k) for source in range(c...]
    all_to_all x1 -> x2, waiting for transfers between devices: 98 us -> 38.2 us  [exchange(): return lax.all_to_all(values, axes, split_axis=0, concat_axis=0, tiled=True)]
    pallas_call x3 -> x5, Pallas kernels: 40.6 us -> 50.1 us  [the longest x2 25.9 us: middle(): pl.pallas_call(body, grid=(1,), in_specs=[scalar, scalar] + [whole(t.shap...]
    unnamed x0 -> x164, local copies, waits for them, and re-layouts: none -> 3.6 us
    all_to_all x1 -> x2, starting transfers between devices: 7.44 us -> 10.3 us  [exchange(): return lax.all_to_all(values, axes, split_axis=0, concat_axis=0, tiled=True)]
  transfers between devices with their start and end apart: 1 -> 64, of which waited for: 1 -> 17; matrix products, arithmetic and copies ran while one was open for 0% -> 0% of each run, Pallas kernels for 0% -> 6%
where the time goes in v2:
time: 288 us; the launch traced here: 286 us
  starting transfers between devices  116 us (40%)
  waiting for transfers between devices  115 us (40%)
  Pallas kernels  50.1 us (17%)
  local copies, waits for them, and re-layouts  3.6 us (1%)
    ppermute x62, starting transfers between devices, swap(): lax.ppermute(blocks[k], axes, [(source, source ^ k) for source in range(c...  106 us
    ppermute x62, waiting for transfers between devices, swap(): lax.ppermute(blocks[k], axes, [(source, source ^ k) for source in range(c...  76.4 us
    all_to_all x2, waiting for transfers between devices, exchange(): return lax.all_to_all(values, axes, split_axis=0, concat_axis=0, tiled=True)  38.2 us
    pallas_call x2, Pallas kernels, middle(): pl.pallas_call(body, grid=(1,), in_specs=[scalar, scalar] + [whole(t.shap...  25.9 us
    pallas_call x1, Pallas kernels, back(): pl.pallas_call(functools.partial(rows_back, shares=shares, block=block),...  11.5 us
    pallas_call x1, Pallas kernels, local_fast(): pl.pallas_call(functools.partial(rows_forward, shares=shares, block=block...  11.4 us
    all_to_all x2, starting transfers between devices, exchange(): return lax.all_to_all(values, axes, split_axis=0, concat_axis=0, tiled=True)  10.3 us
  transfers between devices with their start and end apart: 64, of which 17 were waited for; matrix products, arithmetic and copies ran while one was open for 0% of the time, Pallas kernels for 6%

profile of v2, /device:TPU:0, one launch (start us, length us, event | category | flops | bytes accessed | tf_op | source)
XLA Modules:
  0.0 286.0 jit_solution(2098582980053742778)
XLA Ops:
  0.0 11.4 %rows_forward.1 = (f32[32,96,128]{2,1,0:T(8,128)}, f32[168,128]{1,0:T(8,128)}, f32[168,128]{1,0:T(8,128)}, f32[168,128]{1,0:T(8,128)}, f32[168,128]{1,0:T(8,128)...) custom-call(s32[1]{0:T(128)} %bitcast.index_ref.refs_0_, ...), custom_call_target="tpu_custom_call" | custom-call | tf_op jit(solution)/shard_map/rows_forward/pallas_call | solution.py:636
  11.4 7.3 %all-to-all-start = ((f32[32,96,128]{2,1,0:T(8,128)}), f32[32,96,128]{2,1,0:T(8,128)S(1)}, u32[]{:S(2)}, u32[]{:S(2)}) async-start(f32[32,96,128]{2,1,0:T(8,128)} %get-tuple-element.70), calls=%async_computation | async-start | bytes 3145728 | tf_op jit(solution)/shard_map/all_to_all | solution.py:589
  19.4 38.1 %all-to-all-done.refs_2_ = f32[32,96,128]{2,1,0:T(8,128)S(1)} async-done(((f32[32,96,128]{2,1,0:T(8,128)}), f32[32,96,128]{2,1,0:T(8,128)S(1)}, u32[]{:S(2)}, u32[]{:S(2)}) %all-to-all-start) | async-done | bytes 1572896 | tf_op jit(solution)/shard_map/all_to_all | solution.py:589
  58.7 10.9 %shard_map.100 = f32[32,96,128]{2,1,0:T(8,128)} custom-call(s32[1]{0:T(128)} %bitcast.index_ref.refs_0_, f32[1]{0:T(128)S(6)} %copy.11.refs_1_, f32[32,96,128]{2,1,0:T(8,128)} %copy-done.1, bf16[512,512]{1,0:T(8,128)(2,1)} %constant.26.clone.refs_3_.refs_34_, bf16[512,512]{1,0:T(8,128)(2,1)} %constant.27.clone.refs_4_.refs_35_, ...), custom_call_target="tpu_custom_call" | custom-call | tf_op jit(solution)/shard_map/pallas_call | solution.py:676
  69.8 3.0 %all-to-all-start.1 = ((f32[32,96,128]{2,1,0:T(8,128)}), f32[32,96,128]{2,1,0:T(8,128)S(1)}, u32[]{:S(2)}, u32[]{:S(2)}) async-start(f32[32,96,128]{2,1,0:T(8,128)} %shard_map.100), calls=%async_computation.1 | async-start | bytes 3145728 | tf_op jit(solution)/shard_map/all_to_all | solution.py:589
  72.8 1.5 collective-permute-start
  74.3 1.5 collective-permute-start.1
  76.3 2.5 collective-permute-start.3
  78.8 1.4 collective-permute-start.4
  80.2 10.7 %collective-permute-done.refs_3_ = f32[168,128]{1,0:T(8,128)S(1)} collective-permute-done((f32[168,128]{1,0:T(8,128)}, f32[168,128]{1,0:T(8,128)S(1)}, u32[]{:S(2)}, u32[]{:S(2)}) %collective-permute-start) | collective-permute-done | bytes 86048 | tf_op jit(solution)/shard_map/ppermute | solution.py:596
  90.8 1.3 collective-permute-start.5
  92.2 8.9 %collective-permute-done.1.refs_4_ = f32[168,128]{1,0:T(8,128)S(1)} collective-permute-done((f32[168,128]{1,0:T(8,128)}, f32[168,128]{1,0:T(8,128)S(1)}, u32[]{:S(2)}, u32[]{:S(2)}) %collective-permute-start.1) | collective-permute-done | bytes 86048 | tf_op jit(solution)/shard_map/ppermute | solution.py:596
  101.1 4.5 %collective-permute-start.6 = (f32[168,128]{1,0:T(8,128)}, f32[168,128]{1,0:T(8,128)S(1)}, u32[]{:S(2)}, u32[]{:S(2)}) collective-permute-start(f32[168,128]{1,0:T(8,128)} %get-tuple-element.78), channel_id=1, source_target_pairs={{0,7},{1,6},{2,5},{3,4},{4,3},{5,2},{6,1},{7,0},{8,15},{9,14},{10,... | collective-permute-start | bytes 258056 | tf_op jit(solution)/shard_map/ppermute | solution.py:596
  105.6 14.2 %collective-permute-done.3.refs_6_ = f32[168,128]{1,0:T(8,128)S(1)} collective-permute-done((f32[168,128]{1,0:T(8,128)}, f32[168,128]{1,0:T(8,128)S(1)}, u32[]{:S(2)}, u32[]{:S(2)}) %collective-permute-start.3) | collective-permute-done | bytes 86048 | tf_op jit(solution)/shard_map/ppermute | solution.py:596
  119.9 2.7 collective-permute-done.4.refs_7_
  122.6 1.7 collective-permute-start.10
  124.4 1.4 collective-permute-start.11
  125.8 2.3 collective-permute-start.12
  128.6 3.1 %collective-permute-start.14 = (f32[168,128]{1,0:T(8,128)S(1)}, f32[168,128]{1,0:T(8,128)S(1)}, u32[]{:S(2)}, u32[]{:S(2)}) collective-permute-start(f32[168,128]{1,0:T(8,128)S(1)} %copy-done.75), channel_id=1, source_target_pairs={{0,15},{1,14},{2,13},{3,12},{4,11},{5,10},{6,9},{7,8},{8,7},{9,6},... | collective-permute-start | bytes 258056 | tf_op jit(solution)/shard_map/ppermute | solution.py:596
  131.7 1.5 collective-permute-start.15
  133.3 6.7 %collective-permute-start.16 = (f32[168,128]{1,0:T(8,128)S(1)}, f32[168,128]{1,0:T(8,128)S(1)}, u32[]{:S(2)}, u32[]{:S(2)}) collective-permute-start(f32[168,128]{1,0:T(8,128)S(1)} %copy-done.73), channel_id=1, source_target_pairs={{0,17},{1,16},{2,19},{3,18},{4,21},{5,20},{6,23},{7,22},{8,25},{9,... | collective-permute-start | bytes 258056 | tf_op jit(solution)/shard_map/ppermute | solution.py:596
  140.4 3.3 %collective-permute-start.18 = (f32[168,128]{1,0:T(8,128)S(1)}, f32[168,128]{1,0:T(8,128)S(1)}, u32[]{:S(2)}, u32[]{:S(2)}) collective-permute-start(f32[168,128]{1,0:T(8,128)S(1)} %copy-done.71), channel_id=1, source_target_pairs={{0,19},{1,18},{2,17},{3,16},{4,23},{5,22},{6,21},{7,20},{8,27},{9,... | collective-permute-start | bytes 258056 | tf_op jit(solution)/shard_map/ppermute | solution.py:596
  143.7 1.9 collective-permute-start.19
  145.6 2.6 collective-permute-start.20
  148.2 1.6 collective-permute-start.21
  149.8 3.6 %collective-permute-start.22 = (f32[168,128]{1,0:T(8,128)S(1)}, f32[168,128]{1,0:T(8,128)S(1)}, u32[]{:S(2)}, u32[]{:S(2)}) collective-permute-start(f32[168,128]{1,0:T(8,128)S(1)} %copy-done.67), channel_id=1, source_target_pairs={{0,23},{1,22},{2,21},{3,20},{4,19},{5,18},{6,17},{7,16},{8,31},{9,... | collective-permute-start | bytes 258056 | tf_op jit(solution)/shard_map/ppermute | solution.py:596
  153.4 4.4 %collective-permute-done.19.refs_22_ = f32[168,128]{1,0:T(8,128)S(1)} collective-permute-done((f32[168,128]{1,0:T(8,128)S(1)}, f32[168,128]{1,0:T(8,128)S(1)}, u32[]{:S(2)}, u32[]{:S(2)}) %collective-permute-start.19) | collective-permute-done | bytes 86048 | tf_op jit(solution)/shard_map/ppermute | solution.py:596
  158.4 1.3 collective-permute-done.20.refs_23_
  159.7 3.5 %collective-permute-start.26 = (f32[168,128]{1,0:T(8,128)S(1)}, f32[168,128]{1,0:T(8,128)S(1)}, u32[]{:S(2)}, u32[]{:S(2)}) collective-permute-start(f32[168,128]{1,0:T(8,128)S(1)} %copy-done.63), channel_id=1, source_target_pairs={{0,27},{1,26},{2,25},{3,24},{4,31},{5,30},{6,29},{7,28},{8,19},{9,... | collective-permute-start | bytes 258056 | tf_op jit(solution)/shard_map/ppermute | solution.py:596
  163.5 3.4 %collective-permute-start.28 = (f32[168,128]{1,0:T(8,128)S(1)}, f32[168,128]{1,0:T(8,128)S(1)}, u32[]{:S(2)}, u32[]{:S(2)}) collective-permute-start(f32[168,128]{1,0:T(8,128)S(1)} %copy-done.61), channel_id=1, source_target_pairs={{0,29},{1,28},{2,31},{3,30},{4,25},{5,24},{6,27},{7,26},{8,21},{9,... | collective-permute-start | bytes 258056 | tf_op jit(solution)/shard_map/ppermute | solution.py:596
  168.0 4.4 %collective-permute-start.30 = (f32[168,128]{1,0:T(8,128)S(1)}, f32[168,128]{1,0:T(8,128)S(1)}, u32[]{:S(2)}, u32[]{:S(2)}) collective-permute-start(f32[168,128]{1,0:T(8,128)S(1)} %copy-done.59), channel_id=1, source_target_pairs={{0,31},{1,30},{2,29},{3,28},{4,27},{5,26},{6,25},{7,24},{8,23},{9,... | collective-permute-start | bytes 258056 | tf_op jit(solution)/shard_map/ppermute | solution.py:596
  172.4 4.9 %collective-permute-done.27.refs_30_ = f32[168,128]{1,0:T(8,128)S(1)} collective-permute-done((f32[168,128]{1,0:T(8,128)S(1)}, f32[168,128]{1,0:T(8,128)S(1)}, u32[]{:S(2)}, u32[]{:S(2)}) %collective-permute-start.27) | collective-permute-done | bytes 86048 | tf_op jit(solution)/shard_map/ppermute | solution.py:596
  177.3 1.7 collective-permute-done.28.refs_31_
  179.6 15.0 %shard_map.101 = (f32[168,128]{1,0:T(8,128)}, f32[168,128]{1,0:T(8,128)}, f32[168,128]{1,0:T(8,128)}, f32[168,128]{1,0:T(8,128)}, f32[168,128]{1,0:T(8,128)}, /*...) custom-call(s32[1]{0:T(128)} %bitcast.index_ref.refs_0_, ...), custom_call_target="tpu_custom_call" | custom-call | tf_op jit(solution)/shard_map/pallas_call | solution.py:676
  194.7 1.7 collective-permute-start.31
  196.4 4.0 %collective-permute-start.32 = (f32[168,128]{1,0:T(8,128)}, f32[168,128]{1,0:T(8,128)S(1)}, u32[]{:S(2)}, u32[]{:S(2)}) collective-permute-start(f32[168,128]{1,0:T(8,128)} %get-tuple-element.105), channel_id=1, source_target_pairs={{0,2},{1,3},{2,0},{3,1},{4,6},{5,7},{6,4},{7,5},{8,10},{9,11},{10,... | collective-permute-start | bytes 258056 | tf_op jit(solution)/shard_map/ppermute | solution.py:596
  200.4 1.4 collective-permute-start.34
  201.8 2.5 collective-permute-start.35
  204.2 1.5 collective-permute-start.36
  205.7 2.4 collective-permute-start.37
  208.1 6.1 %collective-permute-done.34.refs_4_ = f32[168,128]{1,0:T(8,128)S(1)} collective-permute-done((f32[168,128]{1,0:T(8,128)}, f32[168,128]{1,0:T(8,128)S(1)}, u32[]{:S(2)}, u32[]{:S(2)}) %collective-permute-start.34) | collective-permute-done | bytes 86048 | tf_op jit(solution)/shard_map/ppermute | solution.py:596
  214.1 2.7 collective-permute-done.35.refs_5_
  216.8 1.8 collective-permute-start.41
  219.6 2.5 collective-permute-start.43
  222.1 1.2 collective-permute-start.44
  223.3 2.4 collective-permute-start.45
  225.8 1.3 collective-permute-start.46
  227.1 4.2 %collective-permute-done.42.refs_12_ = f32[168,128]{1,0:T(8,128)S(1)} collective-permute-done((f32[168,128]{1,0:T(8,128)}, f32[168,128]{1,0:T(8,128)S(1)}, u32[]{:S(2)}, u32[]{:S(2)}) %collective-permute-start.42) | collective-permute-done | bytes 86048 | tf_op jit(solution)/shard_map/ppermute | solution.py:596
  231.3 2.0 collective-permute-start.47
  233.2 1.2 collective-permute-done.43.refs_13_
  234.5 2.4 collective-permute-start.49
  236.9 2.8 collective-permute-start.50
  239.8 2.4 collective-permute-start.51
  242.2 2.4 collective-permute-start.52
  244.5 1.9 collective-permute-start.53
  246.4 4.5 %collective-permute-done.50.refs_20_ = f32[168,128]{1,0:T(8,128)S(1)} collective-permute-done((f32[168,128]{1,0:T(8,128)}, f32[168,128]{1,0:T(8,128)S(1)}, u32[]{:S(2)}, u32[]{:S(2)}) %collective-permute-start.50) | collective-permute-done | bytes 86048 | tf_op jit(solution)/shard_map/ppermute | solution.py:596
  250.9 3.6 %collective-permute-done.51.refs_21_ = f32[168,128]{1,0:T(8,128)S(1)} collective-permute-done((f32[168,128]{1,0:T(8,128)}, f32[168,128]{1,0:T(8,128)S(1)}, u32[]{:S(2)}, u32[]{:S(2)}) %collective-permute-start.51) | collective-permute-done | bytes 86048 | tf_op jit(solution)/shard_map/ppermute | solution.py:596
  254.5 2.6 collective-permute-start.57
  257.9 3.7 %collective-permute-start.59 = (f32[168,128]{1,0:T(8,128)}, f32[168,128]{1,0:T(8,128)}, u32[]{:S(2)}, u32[]{:S(2)}) collective-permute-start(f32[168,128]{1,0:T(8,128)} %get-tuple-element.132), channel_id=1, source_target_pairs={{0,29},{1,28},{2,31},{3,30},{4,25},{5,24},{6,27},{7,26},{8,21},{9,... | collective-permute-start | bytes 258056 | tf_op jit(solution)/shard_map/ppermute | solution.py:596
  261.6 1.7 collective-permute-start.60
  263.9 2.7 collective-permute-start.61
  267.8 1.3 near_token.1.refs_32_
  269.1 5.0 %collective-permute-done.59.refs_29_ = f32[168,128]{1,0:T(8,128)} collective-permute-done((f32[168,128]{1,0:T(8,128)}, f32[168,128]{1,0:T(8,128)}, u32[]{:S(2)}, u32[]{:S(2)}) %collective-permute-start.59) | collective-permute-done | bytes 86048 | tf_op jit(solution)/shard_map/ppermute | solution.py:596
  274.3 11.5 %rows_back.1 = f32[3,1,128,4096]{3,2,1,0:T(8,128)} custom-call(s32[1]{0:T(128)} %bitcast.index_ref.refs_0_, f32[32,96,128]{2,1,0:T(8,128)} %copy-done, bf16[384,512]{1,0:T(8,128)(2,1)} %constant.22.clone.high_ref, bf16[384,512]{1,0:T(8,128)(2,1)} %constant.23.clone.low_ref, f32[16,256]{1,0:T(8,128)} %constant.24.clone.cos_ref.refs_5_.refs_36_, ...), custom_call_target="tpu_custom_call" | custom-call | tf_op jit(solution)/shard_map/rows_back/pallas_call | solution.py:691
  (233 shorter events, 8.8 us)
Async XLA Ops:
  11.4 46.1 %all-to-all-start = ((f32[32,96,128]{2,1,0:T(8,128)}), f32[32,96,128]{2,1,0:T(8,128)S(1)}, u32[]{:S(2)}, u32[]{:S(2)}) async-start(f32[32,96,128]{2,1,0:T(8,128)} %get-tuple-element.70), calls=%async_computation | async-start | bytes 3145728 | tf_op jit(solution)/shard_map/all_to_all | solution.py:589
  69.8 196.9 %all-to-all-start.1 = ((f32[32,96,128]{2,1,0:T(8,128)}), f32[32,96,128]{2,1,0:T(8,128)S(1)}, u32[]{:S(2)}, u32[]{:S(2)}) async-start(f32[32,96,128]{2,1,0:T(8,128)} %shard_map.100), calls=%async_computation.1 | async-start | bytes 3145728 | tf_op jit(solution)/shard_map/all_to_all | solution.py:589
  72.8 18.1 %collective-permute-start = (f32[168,128]{1,0:T(8,128)}, f32[168,128]{1,0:T(8,128)S(1)}, u32[]{:S(2)}, u32[]{:S(2)}) collective-permute-start(f32[168,128]{1,0:T(8,128)} %get-tuple-element.72), channel_id=1, source_target_pairs={{0,1},{1,0},{2,3},{3,2},{4,5},{5,4},{6,7},{7,6},{8,9},{9,8},{10,11... | collective-permute-start | bytes 258056 | tf_op jit(solution)/shard_map/ppermute | solution.py:596
  74.3 26.7 %collective-permute-start.1 = (f32[168,128]{1,0:T(8,128)}, f32[168,128]{1,0:T(8,128)S(1)}, u32[]{:S(2)}, u32[]{:S(2)}) collective-permute-start(f32[168,128]{1,0:T(8,128)} %get-tuple-element.73), channel_id=1, source_target_pairs={{0,2},{1,3},{2,0},{3,1},{4,6},{5,7},{6,4},{7,5},{8,10},{9,11},{10,... | collective-permute-start | bytes 258056 | tf_op jit(solution)/shard_map/ppermute | solution.py:596
  75.9 29.7 %collective-permute-start.2 = (f32[168,128]{1,0:T(8,128)}, f32[168,128]{1,0:T(8,128)S(1)}, u32[]{:S(2)}, u32[]{:S(2)}) collective-permute-start(f32[168,128]{1,0:T(8,128)} %get-tuple-element.74), channel_id=1, source_target_pairs={{0,3},{1,2},{2,1},{3,0},{4,7},{5,6},{6,5},{7,4},{8,11},{9,10},{10,... | collective-permute-start | bytes 258056 | tf_op jit(solution)/shard_map/ppermute | solution.py:596
  76.3 43.5 %collective-permute-start.3 = (f32[168,128]{1,0:T(8,128)}, f32[168,128]{1,0:T(8,128)S(1)}, u32[]{:S(2)}, u32[]{:S(2)}) collective-permute-start(f32[168,128]{1,0:T(8,128)} %get-tuple-element.75), channel_id=1, source_target_pairs={{0,4},{1,5},{2,6},{3,7},{4,0},{5,1},{6,2},{7,3},{8,12},{9,13},{10,... | collective-permute-start | bytes 258056 | tf_op jit(solution)/shard_map/ppermute | solution.py:596
  78.8 43.8 %collective-permute-start.4 = (f32[168,128]{1,0:T(8,128)}, f32[168,128]{1,0:T(8,128)S(1)}, u32[]{:S(2)}, u32[]{:S(2)}) collective-permute-start(f32[168,128]{1,0:T(8,128)} %get-tuple-element.76), channel_id=1, source_target_pairs={{0,5},{1,4},{2,7},{3,6},{4,1},{5,0},{6,3},{7,2},{8,13},{9,12},{10,... | collective-permute-start | bytes 258056 | tf_op jit(solution)/shard_map/ppermute | solution.py:596
  90.8 31.8 %collective-permute-start.5 = (f32[168,128]{1,0:T(8,128)}, f32[168,128]{1,0:T(8,128)S(1)}, u32[]{:S(2)}, u32[]{:S(2)}) collective-permute-start(f32[168,128]{1,0:T(8,128)} %get-tuple-element.77), channel_id=1, source_target_pairs={{0,6},{1,7},{2,4},{3,5},{4,2},{5,3},{6,0},{7,1},{8,14},{9,15},{10,... | collective-permute-start | bytes 258056 | tf_op jit(solution)/shard_map/ppermute | solution.py:596
  101.1 23.3 %collective-permute-start.6 = (f32[168,128]{1,0:T(8,128)}, f32[168,128]{1,0:T(8,128)S(1)}, u32[]{:S(2)}, u32[]{:S(2)}) collective-permute-start(f32[168,128]{1,0:T(8,128)} %get-tuple-element.78), channel_id=1, source_target_pairs={{0,7},{1,6},{2,5},{3,4},{4,3},{5,2},{6,1},{7,0},{8,15},{9,14},{10,... | collective-permute-start | bytes 258056 | tf_op jit(solution)/shard_map/ppermute | solution.py:596
  105.6 20.2 %collective-permute-start.7 = (f32[168,128]{1,0:T(8,128)}, f32[168,128]{1,0:T(8,128)S(1)}, u32[]{:S(2)}, u32[]{:S(2)}) collective-permute-start(f32[168,128]{1,0:T(8,128)} %get-tuple-element.79), channel_id=1, source_target_pairs={{0,8},{1,9},{2,10},{3,11},{4,12},{5,13},{6,14},{7,15},{8,0},{9,1},... | collective-permute-start | bytes 258056 | tf_op jit(solution)/shard_map/ppermute | solution.py:596
  119.8 8.3 %collective-permute-start.8 = (f32[168,128]{1,0:T(8,128)S(1)}, f32[168,128]{1,0:T(8,128)S(1)}, u32[]{:S(2)}, u32[]{:S(2)}) collective-permute-start(f32[168,128]{1,0:T(8,128)S(1)} %copy-done.81), channel_id=1, source_target_pairs={{0,9},{1,8},{2,11},{3,10},{4,13},{5,12},{6,15},{7,14},{8,1},{9,0},... | collective-permute-start | bytes 258056 | tf_op jit(solution)/shard_map/ppermute | solution.py:596
  122.6 6.0 %collective-permute-start.9 = (f32[168,128]{1,0:T(8,128)S(1)}, f32[168,128]{1,0:T(8,128)S(1)}, u32[]{:S(2)}, u32[]{:S(2)}) collective-permute-start(f32[168,128]{1,0:T(8,128)S(1)} %copy-done.80), channel_id=1, source_target_pairs={{0,10},{1,11},{2,8},{3,9},{4,14},{5,15},{6,12},{7,13},{8,2},{9,3},... | collective-permute-start | bytes 258056 | tf_op jit(solution)/shard_map/ppermute | solution.py:596
  122.6 9.1 %collective-permute-start.10 = (f32[168,128]{1,0:T(8,128)S(1)}, f32[168,128]{1,0:T(8,128)S(1)}, u32[]{:S(2)}, u32[]{:S(2)}) collective-permute-start(f32[168,128]{1,0:T(8,128)S(1)} %copy-done.79), channel_id=1, source_target_pairs={{0,11},{1,10},{2,9},{3,8},{4,15},{5,14},{6,13},{7,12},{8,3},{9,2},... | collective-permute-start | bytes 258056 | tf_op jit(solution)/shard_map/ppermute | solution.py:596
  124.4 8.9 %collective-permute-start.11 = (f32[168,128]{1,0:T(8,128)S(1)}, f32[168,128]{1,0:T(8,128)S(1)}, u32[]{:S(2)}, u32[]{:S(2)}) collective-permute-start(f32[168,128]{1,0:T(8,128)S(1)} %copy-done.78), channel_id=1, source_target_pairs={{0,12},{1,13},{2,14},{3,15},{4,8},{5,9},{6,10},{7,11},{8,4},{9,5},... | collective-permute-start | bytes 258056 | tf_op jit(solution)/shard_map/ppermute | solution.py:596
  125.8 14.5 %collective-permute-start.12 = (f32[168,128]{1,0:T(8,128)S(1)}, f32[168,128]{1,0:T(8,128)S(1)}, u32[]{:S(2)}, u32[]{:S(2)}) collective-permute-start(f32[168,128]{1,0:T(8,128)S(1)} %copy-done.77), channel_id=1, source_target_pairs={{0,13},{1,12},{2,15},{3,14},{4,9},{5,8},{6,11},{7,10},{8,5},{9,4},... | collective-permute-start | bytes 258056 | tf_op jit(solution)/shard_map/ppermute | solution.py:596
  128.1 12.2 %collective-permute-start.13 = (f32[168,128]{1,0:T(8,128)S(1)}, f32[168,128]{1,0:T(8,128)S(1)}, u32[]{:S(2)}, u32[]{:S(2)}) collective-permute-start(f32[168,128]{1,0:T(8,128)S(1)} %copy-done.76), channel_id=1, source_target_pairs={{0,14},{1,15},{2,12},{3,13},{4,10},{5,11},{6,8},{7,9},{8,6},{9,7},... | collective-permute-start | bytes 258056 | tf_op jit(solution)/shard_map/ppermute | solution.py:596
  128.6 15.1 %collective-permute-start.14 = (f32[168,128]{1,0:T(8,128)S(1)}, f32[168,128]{1,0:T(8,128)S(1)}, u32[]{:S(2)}, u32[]{:S(2)}) collective-permute-start(f32[168,128]{1,0:T(8,128)S(1)} %copy-done.75), channel_id=1, source_target_pairs={{0,15},{1,14},{2,13},{3,12},{4,11},{5,10},{6,9},{7,8},{8,7},{9,6},... | collective-permute-start | bytes 258056 | tf_op jit(solution)/shard_map/ppermute | solution.py:596
  131.7 13.8 %collective-permute-start.15 = (f32[168,128]{1,0:T(8,128)S(1)}, f32[168,128]{1,0:T(8,128)S(1)}, u32[]{:S(2)}, u32[]{:S(2)}) collective-permute-start(f32[168,128]{1,0:T(8,128)S(1)} %copy-done.74), channel_id=1, source_target_pairs={{0,16},{1,17},{2,18},{3,19},{4,20},{5,21},{6,22},{7,23},{8,24},{9,... | collective-permute-start | bytes 258056 | tf_op jit(solution)/shard_map/ppermute | solution.py:596
  133.3 14.9 %collective-permute-start.16 = (f32[168,128]{1,0:T(8,128)S(1)}, f32[168,128]{1,0:T(8,128)S(1)}, u32[]{:S(2)}, u32[]{:S(2)}) collective-permute-start(f32[168,128]{1,0:T(8,128)S(1)} %copy-done.73), channel_id=1, source_target_pairs={{0,17},{1,16},{2,19},{3,18},{4,21},{5,20},{6,23},{7,22},{8,25},{9,... | collective-permute-start | bytes 258056 | tf_op jit(solution)/shard_map/ppermute | solution.py:596
  140.3 9.5 %collective-permute-start.17 = (f32[168,128]{1,0:T(8,128)S(1)}, f32[168,128]{1,0:T(8,128)S(1)}, u32[]{:S(2)}, u32[]{:S(2)}) collective-permute-start(f32[168,128]{1,0:T(8,128)S(1)} %copy-done.72), channel_id=1, source_target_pairs={{0,18},{1,19},{2,16},{3,17},{4,22},{5,23},{6,20},{7,21},{8,26},{9,... | collective-permute-start | bytes 258056 | tf_op jit(solution)/shard_map/ppermute | solution.py:596
  140.4 13.0 %collective-permute-start.18 = (f32[168,128]{1,0:T(8,128)S(1)}, f32[168,128]{1,0:T(8,128)S(1)}, u32[]{:S(2)}, u32[]{:S(2)}) collective-permute-start(f32[168,128]{1,0:T(8,128)S(1)} %copy-done.71), channel_id=1, source_target_pairs={{0,19},{1,18},{2,17},{3,16},{4,23},{5,22},{6,21},{7,20},{8,27},{9,... | collective-permute-start | bytes 258056 | tf_op jit(solution)/shard_map/ppermute | solution.py:596
  143.7 14.2 %collective-permute-start.19 = (f32[168,128]{1,0:T(8,128)S(1)}, f32[168,128]{1,0:T(8,128)S(1)}, u32[]{:S(2)}, u32[]{:S(2)}) collective-permute-start(f32[168,128]{1,0:T(8,128)S(1)} %copy-done.70), channel_id=1, source_target_pairs={{0,20},{1,21},{2,22},{3,23},{4,16},{5,17},{6,18},{7,19},{8,28},{9,... | collective-permute-start | bytes 258056 | tf_op jit(solution)/shard_map/ppermute | solution.py:596
  145.6 14.1 %collective-permute-start.20 = (f32[168,128]{1,0:T(8,128)S(1)}, f32[168,128]{1,0:T(8,128)S(1)}, u32[]{:S(2)}, u32[]{:S(2)}) collective-permute-start(f32[168,128]{1,0:T(8,128)S(1)} %copy-done.69), channel_id=1, source_target_pairs={{0,21},{1,20},{2,23},{3,22},{4,17},{5,16},{6,19},{7,18},{8,29},{9,... | collective-permute-start | bytes 258056 | tf_op jit(solution)/shard_map/ppermute | solution.py:596
  148.2 11.5 %collective-permute-start.21 = (f32[168,128]{1,0:T(8,128)S(1)}, f32[168,128]{1,0:T(8,128)S(1)}, u32[]{:S(2)}, u32[]{:S(2)}) collective-permute-start(f32[168,128]{1,0:T(8,128)S(1)} %copy-done.68), channel_id=1, source_target_pairs={{0,22},{1,23},{2,20},{3,21},{4,18},{5,19},{6,16},{7,17},{8,30},{9,... | collective-permute-start | bytes 258056 | tf_op jit(solution)/shard_map/ppermute | solution.py:596
  149.8 13.4 %collective-permute-start.22 = (f32[168,128]{1,0:T(8,128)S(1)}, f32[168,128]{1,0:T(8,128)S(1)}, u32[]{:S(2)}, u32[]{:S(2)}) collective-permute-start(f32[168,128]{1,0:T(8,128)S(1)} %copy-done.67), channel_id=1, source_target_pairs={{0,23},{1,22},{2,21},{3,20},{4,19},{5,18},{6,17},{7,16},{8,31},{9,... | collective-permute-start | bytes 258056 | tf_op jit(solution)/shard_map/ppermute | solution.py:596
  153.4 10.2 %collective-permute-start.23 = (f32[168,128]{1,0:T(8,128)S(1)}, f32[168,128]{1,0:T(8,128)S(1)}, u32[]{:S(2)}, u32[]{:S(2)}) collective-permute-start(f32[168,128]{1,0:T(8,128)S(1)} %copy-done.66), channel_id=1, source_target_pairs={{0,24},{1,25},{2,26},{3,27},{4,28},{5,29},{6,30},{7,31},{8,16},{9,... | collective-permute-start | bytes 258056 | tf_op jit(solution)/shard_map/ppermute | solution.py:596
  157.8 9.1 %collective-permute-start.24 = (f32[168,128]{1,0:T(8,128)S(1)}, f32[168,128]{1,0:T(8,128)S(1)}, u32[]{:S(2)}, u32[]{:S(2)}) collective-permute-start(f32[168,128]{1,0:T(8,128)S(1)} %copy-done.65), channel_id=1, source_target_pairs={{0,25},{1,24},{2,27},{3,26},{4,29},{5,28},{6,31},{7,30},{8,17},{9,... | collective-permute-start | bytes 258056 | tf_op jit(solution)/shard_map/ppermute | solution.py:596
  159.7 8.3 %collective-permute-start.25 = (f32[168,128]{1,0:T(8,128)S(1)}, f32[168,128]{1,0:T(8,128)S(1)}, u32[]{:S(2)}, u32[]{:S(2)}) collective-permute-start(f32[168,128]{1,0:T(8,128)S(1)} %copy-done.64), channel_id=1, source_target_pairs={{0,26},{1,27},{2,24},{3,25},{4,30},{5,31},{6,28},{7,29},{8,18},{9,... | collective-permute-start | bytes 258056 | tf_op jit(solution)/shard_map/ppermute | solution.py:596
  159.7 12.6 %collective-permute-start.26 = (f32[168,128]{1,0:T(8,128)S(1)}, f32[168,128]{1,0:T(8,128)S(1)}, u32[]{:S(2)}, u32[]{:S(2)}) collective-permute-start(f32[168,128]{1,0:T(8,128)S(1)} %copy-done.63), channel_id=1, source_target_pairs={{0,27},{1,26},{2,25},{3,24},{4,31},{5,30},{6,29},{7,28},{8,19},{9,... | collective-permute-start | bytes 258056 | tf_op jit(solution)/shard_map/ppermute | solution.py:596
  163.2 14.1 %collective-permute-start.27 = (f32[168,128]{1,0:T(8,128)S(1)}, f32[168,128]{1,0:T(8,128)S(1)}, u32[]{:S(2)}, u32[]{:S(2)}) collective-permute-start(f32[168,128]{1,0:T(8,128)S(1)} %copy-done.62), channel_id=1, source_target_pairs={{0,28},{1,29},{2,30},{3,31},{4,24},{5,25},{6,26},{7,27},{8,20},{9,... | collective-permute-start | bytes 258056 | tf_op jit(solution)/shard_map/ppermute | solution.py:596
  163.5 15.4 %collective-permute-start.28 = (f32[168,128]{1,0:T(8,128)S(1)}, f32[168,128]{1,0:T(8,128)S(1)}, u32[]{:S(2)}, u32[]{:S(2)}) collective-permute-start(f32[168,128]{1,0:T(8,128)S(1)} %copy-done.61), channel_id=1, source_target_pairs={{0,29},{1,28},{2,31},{3,30},{4,25},{5,24},{6,27},{7,26},{8,21},{9,... | collective-permute-start | bytes 258056 | tf_op jit(solution)/shard_map/ppermute | solution.py:596
  167.0 12.0 %collective-permute-start.29 = (f32[168,128]{1,0:T(8,128)S(1)}, f32[168,128]{1,0:T(8,128)S(1)}, u32[]{:S(2)}, u32[]{:S(2)}) collective-permute-start(f32[168,128]{1,0:T(8,128)S(1)} %copy-done.60), channel_id=1, source_target_pairs={{0,30},{1,31},{2,28},{3,29},{4,26},{5,27},{6,24},{7,25},{8,22},{9,... | collective-permute-start | bytes 258056 | tf_op jit(solution)/shard_map/ppermute | solution.py:596
  168.0 10.9 %collective-permute-start.30 = (f32[168,128]{1,0:T(8,128)S(1)}, f32[168,128]{1,0:T(8,128)S(1)}, u32[]{:S(2)}, u32[]{:S(2)}) collective-permute-start(f32[168,128]{1,0:T(8,128)S(1)} %copy-done.59), channel_id=1, source_target_pairs={{0,31},{1,30},{2,29},{3,28},{4,27},{5,26},{6,25},{7,24},{8,23},{9,... | collective-permute-start | bytes 258056 | tf_op jit(solution)/shard_map/ppermute | solution.py:596
  194.7 9.5 %collective-permute-start.31 = (f32[168,128]{1,0:T(8,128)}, f32[168,128]{1,0:T(8,128)S(1)}, u32[]{:S(2)}, u32[]{:S(2)}) collective-permute-start(f32[168,128]{1,0:T(8,128)} %get-tuple-element.104), channel_id=1, source_target_pairs={{0,1},{1,0},{2,3},{3,2},{4,5},{5,4},{6,7},{7,6},{8,9},{9,8},{10,11... | collective-permute-start | bytes 258056 | tf_op jit(solution)/shard_map/ppermute | solution.py:596
  196.4 9.3 %collective-permute-start.32 = (f32[168,128]{1,0:T(8,128)}, f32[168,128]{1,0:T(8,128)S(1)}, u32[]{:S(2)}, u32[]{:S(2)}) collective-permute-start(f32[168,128]{1,0:T(8,128)} %get-tuple-element.105), channel_id=1, source_target_pairs={{0,2},{1,3},{2,0},{3,1},{4,6},{5,7},{6,4},{7,5},{8,10},{9,11},{10,... | collective-permute-start | bytes 258056 | tf_op jit(solution)/shard_map/ppermute | solution.py:596
  200.4 7.7 %collective-permute-start.33 = (f32[168,128]{1,0:T(8,128)}, f32[168,128]{1,0:T(8,128)S(1)}, u32[]{:S(2)}, u32[]{:S(2)}) collective-permute-start(f32[168,128]{1,0:T(8,128)} %get-tuple-element.106), channel_id=1, source_target_pairs={{0,3},{1,2},{2,1},{3,0},{4,7},{5,6},{6,5},{7,4},{8,11},{9,10},{10,... | collective-permute-start | bytes 258056 | tf_op jit(solution)/shard_map/ppermute | solution.py:596
  200.4 13.7 %collective-permute-start.34 = (f32[168,128]{1,0:T(8,128)}, f32[168,128]{1,0:T(8,128)S(1)}, u32[]{:S(2)}, u32[]{:S(2)}) collective-permute-start(f32[168,128]{1,0:T(8,128)} %get-tuple-element.107), channel_id=1, source_target_pairs={{0,4},{1,5},{2,6},{3,7},{4,0},{5,1},{6,2},{7,3},{8,12},{9,13},{10,... | collective-permute-start | bytes 258056 | tf_op jit(solution)/shard_map/ppermute | solution.py:596
  201.8 15.0 %collective-permute-start.35 = (f32[168,128]{1,0:T(8,128)}, f32[168,128]{1,0:T(8,128)S(1)}, u32[]{:S(2)}, u32[]{:S(2)}) collective-permute-start(f32[168,128]{1,0:T(8,128)} %get-tuple-element.108), channel_id=1, source_target_pairs={{0,5},{1,4},{2,7},{3,6},{4,1},{5,0},{6,3},{7,2},{8,13},{9,12},{10,... | collective-permute-start | bytes 258056 | tf_op jit(solution)/shard_map/ppermute | solution.py:596
  204.2 12.6 %collective-permute-start.36 = (f32[168,128]{1,0:T(8,128)}, f32[168,128]{1,0:T(8,128)S(1)}, u32[]{:S(2)}, u32[]{:S(2)}) collective-permute-start(f32[168,128]{1,0:T(8,128)} %get-tuple-element.109), channel_id=1, source_target_pairs={{0,6},{1,7},{2,4},{3,5},{4,2},{5,3},{6,0},{7,1},{8,14},{9,15},{10,... | collective-permute-start | bytes 258056 | tf_op jit(solution)/shard_map/ppermute | solution.py:596
  205.7 13.0 %collective-permute-start.37 = (f32[168,128]{1,0:T(8,128)}, f32[168,128]{1,0:T(8,128)S(1)}, u32[]{:S(2)}, u32[]{:S(2)}) collective-permute-start(f32[168,128]{1,0:T(8,128)} %get-tuple-element.110), channel_id=1, source_target_pairs={{0,7},{1,6},{2,5},{3,4},{4,3},{5,2},{6,1},{7,0},{8,15},{9,14},{10,... | collective-permute-start | bytes 258056 | tf_op jit(solution)/shard_map/ppermute | solution.py:596
  208.1 11.5 %collective-permute-start.38 = (f32[168,128]{1,0:T(8,128)}, f32[168,128]{1,0:T(8,128)S(1)}, u32[]{:S(2)}, u32[]{:S(2)}) collective-permute-start(f32[168,128]{1,0:T(8,128)} %get-tuple-element.111), channel_id=1, source_target_pairs={{0,8},{1,9},{2,10},{3,11},{4,12},{5,13},{6,14},{7,15},{8,0},{9,1},... | collective-permute-start | bytes 258056 | tf_op jit(solution)/shard_map/ppermute | solution.py:596
  214.1 8.0 %collective-permute-start.39 = (f32[168,128]{1,0:T(8,128)}, f32[168,128]{1,0:T(8,128)S(1)}, u32[]{:S(2)}, u32[]{:S(2)}) collective-permute-start(f32[168,128]{1,0:T(8,128)} %get-tuple-element.112), channel_id=1, source_target_pairs={{0,9},{1,8},{2,11},{3,10},{4,13},{5,12},{6,15},{7,14},{8,1},{9,0},... | collective-permute-start | bytes 258056 | tf_op jit(solution)/shard_map/ppermute | solution.py:596
  216.8 6.5 %collective-permute-start.40 = (f32[168,128]{1,0:T(8,128)}, f32[168,128]{1,0:T(8,128)S(1)}, u32[]{:S(2)}, u32[]{:S(2)}) collective-permute-start(f32[168,128]{1,0:T(8,128)} %get-tuple-element.113), channel_id=1, source_target_pairs={{0,10},{1,11},{2,8},{3,9},{4,14},{5,15},{6,12},{7,13},{8,2},{9,3},... | collective-permute-start | bytes 258056 | tf_op jit(solution)/shard_map/ppermute | solution.py:596
  216.8 8.9 %collective-permute-start.41 = (f32[168,128]{1,0:T(8,128)}, f32[168,128]{1,0:T(8,128)S(1)}, u32[]{:S(2)}, u32[]{:S(2)}) collective-permute-start(f32[168,128]{1,0:T(8,128)} %get-tuple-element.114), channel_id=1, source_target_pairs={{0,11},{1,10},{2,9},{3,8},{4,15},{5,14},{6,13},{7,12},{8,3},{9,2},... | collective-permute-start | bytes 258056 | tf_op jit(solution)/shard_map/ppermute | solution.py:596
  218.6 12.6 %collective-permute-start.42 = (f32[168,128]{1,0:T(8,128)}, f32[168,128]{1,0:T(8,128)S(1)}, u32[]{:S(2)}, u32[]{:S(2)}) collective-permute-start(f32[168,128]{1,0:T(8,128)} %get-tuple-element.115), channel_id=1, source_target_pairs={{0,12},{1,13},{2,14},{3,15},{4,8},{5,9},{6,10},{7,11},{8,4},{9,5},... | collective-permute-start | bytes 258056 | tf_op jit(solution)/shard_map/ppermute | solution.py:596
  219.6 14.9 %collective-permute-start.43 = (f32[168,128]{1,0:T(8,128)}, f32[168,128]{1,0:T(8,128)S(1)}, u32[]{:S(2)}, u32[]{:S(2)}) collective-permute-start(f32[168,128]{1,0:T(8,128)} %get-tuple-element.116), channel_id=1, source_target_pairs={{0,13},{1,12},{2,15},{3,14},{4,9},{5,8},{6,11},{7,10},{8,5},{9,4},... | collective-permute-start | bytes 258056 | tf_op jit(solution)/shard_map/ppermute | solution.py:596
  222.1 12.4 %collective-permute-start.44 = (f32[168,128]{1,0:T(8,128)}, f32[168,128]{1,0:T(8,128)S(1)}, u32[]{:S(2)}, u32[]{:S(2)}) collective-permute-start(f32[168,128]{1,0:T(8,128)} %get-tuple-element.117), channel_id=1, source_target_pairs={{0,14},{1,15},{2,12},{3,13},{4,10},{5,11},{6,8},{7,9},{8,6},{9,7},... | collective-permute-start | bytes 258056 | tf_op jit(solution)/shard_map/ppermute | solution.py:596
  223.3 13.6 %collective-permute-start.45 = (f32[168,128]{1,0:T(8,128)}, f32[168,128]{1,0:T(8,128)S(1)}, u32[]{:S(2)}, u32[]{:S(2)}) collective-permute-start(f32[168,128]{1,0:T(8,128)} %get-tuple-element.118), channel_id=1, source_target_pairs={{0,15},{1,14},{2,13},{3,12},{4,11},{5,10},{6,9},{7,8},{8,7},{9,6},... | collective-permute-start | bytes 258056 | tf_op jit(solution)/shard_map/ppermute | solution.py:596
  225.8 14.0 %collective-permute-start.46 = (f32[168,128]{1,0:T(8,128)}, f32[168,128]{1,0:T(8,128)S(1)}, u32[]{:S(2)}, u32[]{:S(2)}) collective-permute-start(f32[168,128]{1,0:T(8,128)} %get-tuple-element.119), channel_id=1, source_target_pairs={{0,16},{1,17},{2,18},{3,19},{4,20},{5,21},{6,22},{7,23},{8,24},{9,... | collective-permute-start | bytes 258056 | tf_op jit(solution)/shard_map/ppermute | solution.py:596
  231.3 10.9 %collective-permute-start.47 = (f32[168,128]{1,0:T(8,128)}, f32[168,128]{1,0:T(8,128)S(1)}, u32[]{:S(2)}, u32[]{:S(2)}) collective-permute-start(f32[168,128]{1,0:T(8,128)} %get-tuple-element.120), channel_id=1, source_target_pairs={{0,17},{1,16},{2,19},{3,18},{4,21},{5,20},{6,23},{7,22},{8,25},{9,... | collective-permute-start | bytes 258056 | tf_op jit(solution)/shard_map/ppermute | solution.py:596
  234.5 10.0 %collective-permute-start.48 = (f32[168,128]{1,0:T(8,128)}, f32[168,128]{1,0:T(8,128)S(1)}, u32[]{:S(2)}, u32[]{:S(2)}) collective-permute-start(f32[168,128]{1,0:T(8,128)} %get-tuple-element.121), channel_id=1, source_target_pairs={{0,18},{1,19},{2,16},{3,17},{4,22},{5,23},{6,20},{7,21},{8,26},{9,... | collective-permute-start | bytes 258056 | tf_op jit(solution)/shard_map/ppermute | solution.py:596
  234.5 11.9 %collective-permute-start.49 = (f32[168,128]{1,0:T(8,128)}, f32[168,128]{1,0:T(8,128)S(1)}, u32[]{:S(2)}, u32[]{:S(2)}) collective-permute-start(f32[168,128]{1,0:T(8,128)} %get-tuple-element.122), channel_id=1, source_target_pairs={{0,19},{1,18},{2,17},{3,16},{4,23},{5,22},{6,21},{7,20},{8,27},{9,... | collective-permute-start | bytes 258056 | tf_op jit(solution)/shard_map/ppermute | solution.py:596
  236.9 14.0 %collective-permute-start.50 = (f32[168,128]{1,0:T(8,128)}, f32[168,128]{1,0:T(8,128)S(1)}, u32[]{:S(2)}, u32[]{:S(2)}) collective-permute-start(f32[168,128]{1,0:T(8,128)} %get-tuple-element.123), channel_id=1, source_target_pairs={{0,20},{1,21},{2,22},{3,23},{4,16},{5,17},{6,18},{7,19},{8,28},{9,... | collective-permute-start | bytes 258056 | tf_op jit(solution)/shard_map/ppermute | solution.py:596
  239.8 14.7 %collective-permute-start.51 = (f32[168,128]{1,0:T(8,128)}, f32[168,128]{1,0:T(8,128)S(1)}, u32[]{:S(2)}, u32[]{:S(2)}) collective-permute-start(f32[168,128]{1,0:T(8,128)} %get-tuple-element.124), channel_id=1, source_target_pairs={{0,21},{1,20},{2,23},{3,22},{4,17},{5,16},{6,19},{7,18},{8,29},{9,... | collective-permute-start | bytes 258056 | tf_op jit(solution)/shard_map/ppermute | solution.py:596
  242.2 12.4 %collective-permute-start.52 = (f32[168,128]{1,0:T(8,128)}, f32[168,128]{1,0:T(8,128)S(1)}, u32[]{:S(2)}, u32[]{:S(2)}) collective-permute-start(f32[168,128]{1,0:T(8,128)} %get-tuple-element.125), channel_id=1, source_target_pairs={{0,22},{1,23},{2,20},{3,21},{4,18},{5,19},{6,16},{7,17},{8,30},{9,... | collective-permute-start | bytes 258056 | tf_op jit(solution)/shard_map/ppermute | solution.py:596
  244.5 12.6 %collective-permute-start.53 = (f32[168,128]{1,0:T(8,128)}, f32[168,128]{1,0:T(8,128)S(1)}, u32[]{:S(2)}, u32[]{:S(2)}) collective-permute-start(f32[168,128]{1,0:T(8,128)} %get-tuple-element.126), channel_id=1, source_target_pairs={{0,23},{1,22},{2,21},{3,20},{4,19},{5,18},{6,17},{7,16},{8,31},{9,... | collective-permute-start | bytes 258056 | tf_op jit(solution)/shard_map/ppermute | solution.py:596
  246.4 11.5 %collective-permute-start.54 = (f32[168,128]{1,0:T(8,128)}, f32[168,128]{1,0:T(8,128)S(1)}, u32[]{:S(2)}, u32[]{:S(2)}) collective-permute-start(f32[168,128]{1,0:T(8,128)} %get-tuple-element.127), channel_id=1, source_target_pairs={{0,24},{1,25},{2,26},{3,27},{4,28},{5,29},{6,30},{7,31},{8,16},{9,... | collective-permute-start | bytes 258056 | tf_op jit(solution)/shard_map/ppermute | solution.py:596
  250.9 10.7 %collective-permute-start.55 = (f32[168,128]{1,0:T(8,128)}, f32[168,128]{1,0:T(8,128)S(1)}, u32[]{:S(2)}, u32[]{:S(2)}) collective-permute-start(f32[168,128]{1,0:T(8,128)} %get-tuple-element.128), channel_id=1, source_target_pairs={{0,25},{1,24},{2,27},{3,26},{4,29},{5,28},{6,31},{7,30},{8,17},{9,... | collective-permute-start | bytes 258056 | tf_op jit(solution)/shard_map/ppermute | solution.py:596
  254.5 8.8 %collective-permute-start.56 = (f32[168,128]{1,0:T(8,128)}, f32[168,128]{1,0:T(8,128)S(1)}, u32[]{:S(2)}, u32[]{:S(2)}) collective-permute-start(f32[168,128]{1,0:T(8,128)} %get-tuple-element.129), channel_id=1, source_target_pairs={{0,26},{1,27},{2,24},{3,25},{4,30},{5,31},{6,28},{7,29},{8,18},{9,... | collective-permute-start | bytes 258056 | tf_op jit(solution)/shard_map/ppermute | solution.py:596
  254.5 14.5 %collective-permute-start.57 = (f32[168,128]{1,0:T(8,128)}, f32[168,128]{1,0:T(8,128)}, u32[]{:S(2)}, u32[]{:S(2)}) collective-permute-start(f32[168,128]{1,0:T(8,128)} %get-tuple-element.130), channel_id=1, source_target_pairs={{0,27},{1,26},{2,25},{3,24},{4,31},{5,30},{6,29},{7,28},{8,19},{9,... | collective-permute-start | bytes 258056 | tf_op jit(solution)/shard_map/ppermute | solution.py:596
  257.1 11.9 %collective-permute-start.58 = (f32[168,128]{1,0:T(8,128)}, f32[168,128]{1,0:T(8,128)}, u32[]{:S(2)}, u32[]{:S(2)}) collective-permute-start(f32[168,128]{1,0:T(8,128)} %get-tuple-element.131), channel_id=1, source_target_pairs={{0,28},{1,29},{2,30},{3,31},{4,24},{5,25},{6,26},{7,27},{8,20},{9,... | collective-permute-start | bytes 258056 | tf_op jit(solution)/shard_map/ppermute | solution.py:596
  257.9 16.2 %collective-permute-start.59 = (f32[168,128]{1,0:T(8,128)}, f32[168,128]{1,0:T(8,128)}, u32[]{:S(2)}, u32[]{:S(2)}) collective-permute-start(f32[168,128]{1,0:T(8,128)} %get-tuple-element.132), channel_id=1, source_target_pairs={{0,29},{1,28},{2,31},{3,30},{4,25},{5,24},{6,27},{7,26},{8,21},{9,... | collective-permute-start | bytes 258056 | tf_op jit(solution)/shard_map/ppermute | solution.py:596
  261.6 12.5 %collective-permute-start.60 = (f32[168,128]{1,0:T(8,128)}, f32[168,128]{1,0:T(8,128)}, u32[]{:S(2)}, u32[]{:S(2)}) collective-permute-start(f32[168,128]{1,0:T(8,128)} %get-tuple-element.133), channel_id=1, source_target_pairs={{0,30},{1,31},{2,28},{3,29},{4,26},{5,27},{6,24},{7,25},{8,22},{9,... | collective-permute-start | bytes 258056 | tf_op jit(solution)/shard_map/ppermute | solution.py:596
  263.9 10.2 %collective-permute-start.61 = (f32[168,128]{1,0:T(8,128)}, f32[168,128]{1,0:T(8,128)}, u32[]{:S(2)}, u32[]{:S(2)}) collective-permute-start(f32[168,128]{1,0:T(8,128)} %get-tuple-element.134), channel_id=1, source_target_pairs={{0,31},{1,30},{2,29},{3,28},{4,27},{5,26},{6,25},{7,24},{8,23},{9,... | collective-permute-start | bytes 258056 | tf_op jit(solution)/shard_map/ppermute | solution.py:596
  (82 other events, 3782.4 us)

commit v3 on v2

--- a/solution.py
+++ b/solution.py
@@ -317,12 +317,26 @@
     return one(left_high, right_high) + one(left_low, right_high) + one(left_high, right_low)
 
 
+def stacked_products(stack_ref, height, high, low):
+    depth = stack_ref.shape[0] // 2
+
+    def one(a, b):
+        return lax.dot_general(a, b, (((1,), (1,)), ((), ())), preferred_element_type=jnp.float32)
+
+    if 2 * height < depth:
+        upper, lower = one(stack_ref[:height], high), one(stack_ref[depth : depth + height], high)
+    else:
+        both = one(stack_ref[...], high)
+        upper, lower = both[:height], both[depth : depth + height]
+    return upper + lower + one(stack_ref[:height], low)
+
+
 def slot_order():
     return [0, radix // 2] + list(range(1, radix // 2))
 
 
 def rows_forward(
-    index_ref, x_ref, high_ref, low_ref, cos_ref, sin_ref, near_ref, *refs, shares, block
+    index_ref, x_ref, stack_ref, cos_ref, sin_ref, near_ref, *refs, shares, block
 ):
     far_refs = refs[:-3]
     th_ref, tl_ref, box_ref = refs[-3:]
@@ -359,16 +373,13 @@
         return carry
 
     lax.fori_loop(0, rows // chunk, vector_stage, 0)
-    nt = ((1,), (1,))
     single = shares * block
     slot = 0
     while slot < len(order):
         count = min(2, len(order) - slot)
         height = single if slot == 0 else 2 * single
         where = slice(slot * rows, (slot + count) * rows)
-        result = three_products(
-            (high_ref[:height], low_ref[:height]), (th_ref[where], tl_ref[where]), nt
-        )
+        result = stacked_products(stack_ref, height, th_ref[where], tl_ref[where])
         for index in range(count):
             s = order[slot + index]
             columns = result[:, index * rows : (index + 1) * rows]
@@ -385,7 +396,7 @@
         far_ref[where, :] = box_ref[index_ref[0] ^ k]
 
 
-def rows_back(index_ref, near_ref, high_ref, low_ref, cos_ref, sin_ref, *refs, shares, block):
+def rows_back(index_ref, near_ref, stack_ref, cos_ref, sin_ref, *refs, shares, block):
     out_ref, g_ref, far_ref = refs[-3:]
     devices, height = far_ref.shape[:2]
     place = pl.ds(pl.program_id(0) * height, height)
@@ -394,6 +405,7 @@
     rows, length = out_ref.shape[2:]
     inner = length // radix
     order = slot_order()
+    depth = stack_ref.shape[0] // 2
     for slot, s in enumerate(order):
         blocks = []
         for residue in [s] if slot < 2 else [s, radix - s]:
@@ -404,11 +416,10 @@
         if wide > used:
             blocks.append(jnp.zeros((wide - used, rows), jnp.float32))
         turned = jnp.transpose(jnp.concatenate(blocks, axis=0))
-        keep = slice(0, wide)
         g_ref[slot * rows : (slot + 1) * rows] = three_products(
-            split_parts(turned), (high_ref[keep], low_ref[keep]), ((1,), (0,))
+            split_parts(turned), (stack_ref[:wide], stack_ref[depth : depth + wide]), ((1,), (0,))
         )
-    chunk = tile
+    chunk = 2 * tile
 
     def vector_stage(step, carry):
         start = pl.multiple_of(step * chunk, chunk)
@@ -449,7 +460,6 @@
     length_y = radix * inner
     chunk = 2 * tile
     padded = -(-lines // chunk) * chunk
-    group = radix * padded
     half = tile // 2
 
     def read(in_ref, c, source, start):
@@ -506,15 +516,13 @@
         base += count
 
     def products(dims):
-        def run(step, carry):
-            c = step // 2
-            where = pl.ds(pl.multiple_of((step % 2) * (group // 2), chunk), group // 2)
-            x_ref[c, where, :] = three_products(
-                (th_ref[c, where, :], tl_ref[c, where, :]), (high_ref[...], low_ref[...]), dims
+        def run(c, carry):
+            x_ref[c] = three_products(
+                (th_ref[c], tl_ref[c]), (high_ref[...], low_ref[...]), dims
             )
             return carry
 
-        lax.fori_loop(0, 2 * components, run, 0)
+        lax.fori_loop(0, components, run, 0)
 
     products(((1,), (0,)))
 
@@ -609,7 +617,7 @@
     table = row_table(inner, per_device, shares, block)
     table = np.pad(table, ((0, -len(table) % lane), (0, 0)))
     line_inner = shares * rows
-    row_tables = [jnp.asarray(t) for t in split_table(table)]
+    row_tables = [jnp.asarray(np.concatenate(split_table(table)))]
     row_tables += [jnp.asarray(t, jnp.float32) for t in twist_table(inner)]
     line_tables = [jnp.asarray(t) for t in split_table(square_table(line_inner))]
     line_tables += [jnp.asarray(t, jnp.float32) for t in twist_table(line_inner)]

time: 288 us -> 284 us (0.986)
  Pallas kernels: 50.1 us -> 46.5 us
    pallas_call x2, Pallas kernels: 25.9 us -> 22.3 us  [middle(): pl.pallas_call(body, grid=(1,), in_specs=[scalar, scalar] + [whole(t.shap...]
  transfers between devices with their start and end apart: 64 -> 64, of which waited for: 17 -> 17; matrix products, arithmetic and copies ran while one was open for 0% -> 0% of each run, Pallas kernels for 6% -> 5%
where the time goes in v3:
time: 284 us; the launch traced here: 282 us
  starting transfers between devices  116 us (41%)
  waiting for transfers between devices  115 us (40%)
  Pallas kernels  46.5 us (16%)
  local copies, waits for them, and re-layouts  3.6 us (1%)
    ppermute x62, starting transfers between devices, swap(): lax.ppermute(blocks[k], axes, [(source, source ^ k) for source in range(c...  106 us
    ppermute x62, waiting for transfers between devices, swap(): lax.ppermute(blocks[k], axes, [(source, source ^ k) for source in range(c...  76.4 us
    all_to_all x2, waiting for transfers between devices, exchange(): return lax.all_to_all(values, axes, split_axis=0, concat_axis=0, tiled=True)  38.2 us
    pallas_call x2, Pallas kernels, middle(): pl.pallas_call(body, grid=(1,), in_specs=[scalar, scalar] + [whole(t.shap...  22.3 us
    pallas_call x1, Pallas kernels, local_fast(): pl.pallas_call(functools.partial(rows_forward, shares=shares, block=block...  11.6 us
    pallas_call x1, Pallas kernels, back(): pl.pallas_call(functools.partial(rows_back, shares=shares, block=block),...  11.4 us
    all_to_all x2, starting transfers between devices, exchange(): return lax.all_to_all(values, axes, split_axis=0, concat_axis=0, tiled=True)  10.4 us
  transfers between devices with their start and end apart: 64, of which 17 were waited for; matrix products, arithmetic and copies ran while one was open for 0% of the time, Pallas kernels for 5%

profile of v3, /device:TPU:0, one launch (start us, length us, event | category | flops | bytes accessed | tf_op | source)
XLA Modules:
  0.0 282.4 jit_solution(3494562079153681063)
XLA Ops:
  0.0 11.6 %rows_forward.1 = (f32[32,96,128]{2,1,0:T(8,128)}, f32[168,128]{1,0:T(8,128)}, f32[168,128]{1,0:T(8,128)}, f32[168,128]{1,0:T(8,128)}, f32[168,128]{1,0:T(8,128)...) custom-call(s32[1]{0:T(128)} %bitcast.index_ref.refs_0_, ...), custom_call_target="tpu_custom_call" | custom-call | tf_op jit(solution)/shard_map/rows_forward/pallas_call | solution.py:644
  11.6 7.3 %all-to-all-start = ((f32[32,96,128]{2,1,0:T(8,128)}), f32[32,96,128]{2,1,0:T(8,128)S(1)}, u32[]{:S(2)}, u32[]{:S(2)}) async-start(f32[32,96,128]{2,1,0:T(8,128)} %get-tuple-element.70), calls=%async_computation | async-start | bytes 3145728 | tf_op jit(solution)/shard_map/all_to_all | solution.py:597
  19.6 38.1 %all-to-all-done.refs_2_ = f32[32,96,128]{2,1,0:T(8,128)S(1)} async-done(((f32[32,96,128]{2,1,0:T(8,128)}), f32[32,96,128]{2,1,0:T(8,128)S(1)}, u32[]{:S(2)}, u32[]{:S(2)}) %all-to-all-start) | async-done | bytes 1572896 | tf_op jit(solution)/shard_map/all_to_all | solution.py:597
  58.9 8.3 %shard_map.91 = f32[32,96,128]{2,1,0:T(8,128)} custom-call(s32[1]{0:T(128)} %bitcast.index_ref.refs_0_, f32[1]{0:T(128)S(6)} %copy.10.refs_1_, f32[32,96,128]{2,1,0:T(8,128)} %copy-done.1, bf16[512,512]{1,0:T(8,128)(2,1)} %constant.23.clone.refs_3_.refs_34_, bf16[512,512]{1,0:T(8,128)(2,1)} %constant.24.clone.refs_4_.refs_35_, ...), custom_call_target="tpu_custom_call" | custom-call | tf_op jit(solution)/shard_map/pallas_call | solution.py:684
  67.4 3.0 %all-to-all-start.1 = ((f32[32,96,128]{2,1,0:T(8,128)}), f32[32,96,128]{2,1,0:T(8,128)S(1)}, u32[]{:S(2)}, u32[]{:S(2)}) async-start(f32[32,96,128]{2,1,0:T(8,128)} %shard_map.91), calls=%async_computation.1 | async-start | bytes 3145728 | tf_op jit(solution)/shard_map/all_to_all | solution.py:597
  70.4 1.5 collective-permute-start
  72.0 1.5 collective-permute-start.1
  74.0 2.5 collective-permute-start.3
  76.5 1.4 collective-permute-start.4
  77.8 10.7 %collective-permute-done.refs_3_ = f32[168,128]{1,0:T(8,128)S(1)} collective-permute-done((f32[168,128]{1,0:T(8,128)}, f32[168,128]{1,0:T(8,128)S(1)}, u32[]{:S(2)}, u32[]{:S(2)}) %collective-permute-start) | collective-permute-done | bytes 86048 | tf_op jit(solution)/shard_map/ppermute | solution.py:604
  88.5 1.3 collective-permute-start.5
  89.8 8.9 %collective-permute-done.1.refs_4_ = f32[168,128]{1,0:T(8,128)S(1)} collective-permute-done((f32[168,128]{1,0:T(8,128)}, f32[168,128]{1,0:T(8,128)S(1)}, u32[]{:S(2)}, u32[]{:S(2)}) %collective-permute-start.1) | collective-permute-done | bytes 86048 | tf_op jit(solution)/shard_map/ppermute | solution.py:604
  98.7 4.5 %collective-permute-start.6 = (f32[168,128]{1,0:T(8,128)}, f32[168,128]{1,0:T(8,128)S(1)}, u32[]{:S(2)}, u32[]{:S(2)}) collective-permute-start(f32[168,128]{1,0:T(8,128)} %get-tuple-element.78), channel_id=1, source_target_pairs={{0,7},{1,6},{2,5},{3,4},{4,3},{5,2},{6,1},{7,0},{8,15},{9,14},{10,... | collective-permute-start | bytes 258056 | tf_op jit(solution)/shard_map/ppermute | solution.py:604
  103.2 14.2 %collective-permute-done.3.refs_6_ = f32[168,128]{1,0:T(8,128)S(1)} collective-permute-done((f32[168,128]{1,0:T(8,128)}, f32[168,128]{1,0:T(8,128)S(1)}, u32[]{:S(2)}, u32[]{:S(2)}) %collective-permute-start.3) | collective-permute-done | bytes 86048 | tf_op jit(solution)/shard_map/ppermute | solution.py:604
  117.5 2.7 collective-permute-done.4.refs_7_
  120.3 1.7 collective-permute-start.10
  122.0 1.4 collective-permute-start.11
  123.5 2.3 collective-permute-start.12
  126.2 3.1 %collective-permute-start.14 = (f32[168,128]{1,0:T(8,128)S(1)}, f32[168,128]{1,0:T(8,128)S(1)}, u32[]{:S(2)}, u32[]{:S(2)}) collective-permute-start(f32[168,128]{1,0:T(8,128)S(1)} %copy-done.75), channel_id=1, source_target_pairs={{0,15},{1,14},{2,13},{3,12},{4,11},{5,10},{6,9},{7,8},{8,7},{9,6},... | collective-permute-start | bytes 258056 | tf_op jit(solution)/shard_map/ppermute | solution.py:604
  129.4 1.5 collective-permute-start.15
  130.9 6.7 %collective-permute-start.16 = (f32[168,128]{1,0:T(8,128)S(1)}, f32[168,128]{1,0:T(8,128)S(1)}, u32[]{:S(2)}, u32[]{:S(2)}) collective-permute-start(f32[168,128]{1,0:T(8,128)S(1)} %copy-done.73), channel_id=1, source_target_pairs={{0,17},{1,16},{2,19},{3,18},{4,21},{5,20},{6,23},{7,22},{8,25},{9,... | collective-permute-start | bytes 258056 | tf_op jit(solution)/shard_map/ppermute | solution.py:604
  138.0 3.3 %collective-permute-start.18 = (f32[168,128]{1,0:T(8,128)S(1)}, f32[168,128]{1,0:T(8,128)S(1)}, u32[]{:S(2)}, u32[]{:S(2)}) collective-permute-start(f32[168,128]{1,0:T(8,128)S(1)} %copy-done.71), channel_id=1, source_target_pairs={{0,19},{1,18},{2,17},{3,16},{4,23},{5,22},{6,21},{7,20},{8,27},{9,... | collective-permute-start | bytes 258056 | tf_op jit(solution)/shard_map/ppermute | solution.py:604
  141.3 1.9 collective-permute-start.19
  143.2 2.6 collective-permute-start.20
  145.8 1.6 collective-permute-start.21
  147.4 3.6 %collective-permute-start.22 = (f32[168,128]{1,0:T(8,128)S(1)}, f32[168,128]{1,0:T(8,128)S(1)}, u32[]{:S(2)}, u32[]{:S(2)}) collective-permute-start(f32[168,128]{1,0:T(8,128)S(1)} %copy-done.67), channel_id=1, source_target_pairs={{0,23},{1,22},{2,21},{3,20},{4,19},{5,18},{6,17},{7,16},{8,31},{9,... | collective-permute-start | bytes 258056 | tf_op jit(solution)/shard_map/ppermute | solution.py:604
  151.1 4.4 %collective-permute-done.19.refs_22_ = f32[168,128]{1,0:T(8,128)S(1)} collective-permute-done((f32[168,128]{1,0:T(8,128)S(1)}, f32[168,128]{1,0:T(8,128)S(1)}, u32[]{:S(2)}, u32[]{:S(2)}) %collective-permute-start.19) | collective-permute-done | bytes 86048 | tf_op jit(solution)/shard_map/ppermute | solution.py:604
  156.0 1.3 collective-permute-done.20.refs_23_
  157.4 3.5 %collective-permute-start.26 = (f32[168,128]{1,0:T(8,128)S(1)}, f32[168,128]{1,0:T(8,128)S(1)}, u32[]{:S(2)}, u32[]{:S(2)}) collective-permute-start(f32[168,128]{1,0:T(8,128)S(1)} %copy-done.63), channel_id=1, source_target_pairs={{0,27},{1,26},{2,25},{3,24},{4,31},{5,30},{6,29},{7,28},{8,19},{9,... | collective-permute-start | bytes 258056 | tf_op jit(solution)/shard_map/ppermute | solution.py:604
  161.2 3.4 %collective-permute-start.28 = (f32[168,128]{1,0:T(8,128)S(1)}, f32[168,128]{1,0:T(8,128)S(1)}, u32[]{:S(2)}, u32[]{:S(2)}) collective-permute-start(f32[168,128]{1,0:T(8,128)S(1)} %copy-done.61), channel_id=1, source_target_pairs={{0,29},{1,28},{2,31},{3,30},{4,25},{5,24},{6,27},{7,26},{8,21},{9,... | collective-permute-start | bytes 258056 | tf_op jit(solution)/shard_map/ppermute | solution.py:604
  165.7 4.4 %collective-permute-start.30 = (f32[168,128]{1,0:T(8,128)S(1)}, f32[168,128]{1,0:T(8,128)S(1)}, u32[]{:S(2)}, u32[]{:S(2)}) collective-permute-start(f32[168,128]{1,0:T(8,128)S(1)} %copy-done.59), channel_id=1, source_target_pairs={{0,31},{1,30},{2,29},{3,28},{4,27},{5,26},{6,25},{7,24},{8,23},{9,... | collective-permute-start | bytes 258056 | tf_op jit(solution)/shard_map/ppermute | solution.py:604
  170.0 4.9 %collective-permute-done.27.refs_30_ = f32[168,128]{1,0:T(8,128)S(1)} collective-permute-done((f32[168,128]{1,0:T(8,128)S(1)}, f32[168,128]{1,0:T(8,128)S(1)}, u32[]{:S(2)}, u32[]{:S(2)}) %collective-permute-start.27) | collective-permute-done | bytes 86048 | tf_op jit(solution)/shard_map/ppermute | solution.py:604
  174.9 1.7 collective-permute-done.28.refs_31_
  177.3 14.0 %shard_map.92 = (f32[168,128]{1,0:T(8,128)}, f32[168,128]{1,0:T(8,128)}, f32[168,128]{1,0:T(8,128)}, f32[168,128]{1,0:T(8,128)}, f32[168,128]{1,0:T(8,128)}, /*i...) custom-call(s32[1]{0:T(128)} %bitcast.index_ref.refs_0_, ...), custom_call_target="tpu_custom_call" | custom-call | tf_op jit(solution)/shard_map/pallas_call | solution.py:684
  191.3 1.7 collective-permute-start.31
  193.0 4.0 %collective-permute-start.32 = (f32[168,128]{1,0:T(8,128)}, f32[168,128]{1,0:T(8,128)S(1)}, u32[]{:S(2)}, u32[]{:S(2)}) collective-permute-start(f32[168,128]{1,0:T(8,128)} %get-tuple-element.105), channel_id=1, source_target_pairs={{0,2},{1,3},{2,0},{3,1},{4,6},{5,7},{6,4},{7,5},{8,10},{9,11},{10,... | collective-permute-start | bytes 258056 | tf_op jit(solution)/shard_map/ppermute | solution.py:604
  197.0 1.4 collective-permute-start.34
  198.3 2.4 collective-permute-start.35
  200.8 1.5 collective-permute-start.36
  202.2 2.4 collective-permute-start.37
  204.6 6.1 %collective-permute-done.34.refs_4_ = f32[168,128]{1,0:T(8,128)S(1)} collective-permute-done((f32[168,128]{1,0:T(8,128)}, f32[168,128]{1,0:T(8,128)S(1)}, u32[]{:S(2)}, u32[]{:S(2)}) %collective-permute-start.34) | collective-permute-done | bytes 86048 | tf_op jit(solution)/shard_map/ppermute | solution.py:604
  210.7 2.6 collective-permute-done.35.refs_5_
  213.4 1.8 collective-permute-start.41
  216.2 2.4 collective-permute-start.43
  218.7 1.2 collective-permute-start.44
  219.9 2.4 collective-permute-start.45
  222.3 1.3 collective-permute-start.46
  223.6 4.2 %collective-permute-done.42.refs_12_ = f32[168,128]{1,0:T(8,128)S(1)} collective-permute-done((f32[168,128]{1,0:T(8,128)}, f32[168,128]{1,0:T(8,128)S(1)}, u32[]{:S(2)}, u32[]{:S(2)}) %collective-permute-start.42) | collective-permute-done | bytes 86048 | tf_op jit(solution)/shard_map/ppermute | solution.py:604
  227.8 2.0 collective-permute-start.47
  229.8 1.2 collective-permute-done.43.refs_13_
  231.1 2.4 collective-permute-start.49
  233.5 2.8 collective-permute-start.50
  236.3 2.4 collective-permute-start.51
  238.7 2.4 collective-permute-start.52
  241.1 1.9 collective-permute-start.53
  243.0 4.5 %collective-permute-done.50.refs_20_ = f32[168,128]{1,0:T(8,128)S(1)} collective-permute-done((f32[168,128]{1,0:T(8,128)}, f32[168,128]{1,0:T(8,128)S(1)}, u32[]{:S(2)}, u32[]{:S(2)}) %collective-permute-start.50) | collective-permute-done | bytes 86048 | tf_op jit(solution)/shard_map/ppermute | solution.py:604
  247.5 3.6 %collective-permute-done.51.refs_21_ = f32[168,128]{1,0:T(8,128)S(1)} collective-permute-done((f32[168,128]{1,0:T(8,128)}, f32[168,128]{1,0:T(8,128)S(1)}, u32[]{:S(2)}, u32[]{:S(2)}) %collective-permute-start.51) | collective-permute-done | bytes 86048 | tf_op jit(solution)/shard_map/ppermute | solution.py:604
  251.1 2.6 collective-permute-start.57
  254.4 3.7 %collective-permute-start.59 = (f32[168,128]{1,0:T(8,128)}, f32[168,128]{1,0:T(8,128)}, u32[]{:S(2)}, u32[]{:S(2)}) collective-permute-start(f32[168,128]{1,0:T(8,128)} %get-tuple-element.132), channel_id=1, source_target_pairs={{0,29},{1,28},{2,31},{3,30},{4,25},{5,24},{6,27},{7,26},{8,21},{9,... | collective-permute-start | bytes 258056 | tf_op jit(solution)/shard_map/ppermute | solution.py:604
  258.2 1.7 collective-permute-start.60
  260.5 2.7 collective-permute-start.61
  264.4 1.3 near_token.1.refs_32_
  265.6 5.0 %collective-permute-done.59.refs_29_ = f32[168,128]{1,0:T(8,128)} collective-permute-done((f32[168,128]{1,0:T(8,128)}, f32[168,128]{1,0:T(8,128)}, u32[]{:S(2)}, u32[]{:S(2)}) %collective-permute-start.59) | collective-permute-done | bytes 86048 | tf_op jit(solution)/shard_map/ppermute | solution.py:604
  270.9 11.4 %rows_back.1 = f32[3,1,128,4096]{3,2,1,0:T(8,128)} custom-call(s32[1]{0:T(128)} %bitcast.index_ref.refs_0_, f32[32,96,128]{2,1,0:T(8,128)} %copy-done, bf16[768,512]{1,0:T(8,128)(2,1)} %constant.20.clone.stack_ref, f32[16,256]{1,0:T(8,128)} %constant.21.clone.cos_ref.refs_5_.refs_36_, f32[16,256]{1,0:T(8,128)} %constant.22.clone.sin_ref.refs_6_.refs_37_, ...), custom_call_target="tpu_custom_call" | custom-call | tf_op jit(solution)/shard_map/rows_back/pallas_call | solution.py:699
  (233 shorter events, 8.9 us)
Async XLA Ops:
  11.6 46.1 %all-to-all-start = ((f32[32,96,128]{2,1,0:T(8,128)}), f32[32,96,128]{2,1,0:T(8,128)S(1)}, u32[]{:S(2)}, u32[]{:S(2)}) async-start(f32[32,96,128]{2,1,0:T(8,128)} %get-tuple-element.70), calls=%async_computation | async-start | bytes 3145728 | tf_op jit(solution)/shard_map/all_to_all | solution.py:597
  67.4 195.8 %all-to-all-start.1 = ((f32[32,96,128]{2,1,0:T(8,128)}), f32[32,96,128]{2,1,0:T(8,128)S(1)}, u32[]{:S(2)}, u32[]{:S(2)}) async-start(f32[32,96,128]{2,1,0:T(8,128)} %shard_map.91), calls=%async_computation.1 | async-start | bytes 3145728 | tf_op jit(solution)/shard_map/all_to_all | solution.py:597
  70.4 18.1 %collective-permute-start = (f32[168,128]{1,0:T(8,128)}, f32[168,128]{1,0:T(8,128)S(1)}, u32[]{:S(2)}, u32[]{:S(2)}) collective-permute-start(f32[168,128]{1,0:T(8,128)} %get-tuple-element.72), channel_id=1, source_target_pairs={{0,1},{1,0},{2,3},{3,2},{4,5},{5,4},{6,7},{7,6},{8,9},{9,8},{10,11... | collective-permute-start | bytes 258056 | tf_op jit(solution)/shard_map/ppermute | solution.py:604
  72.0 26.7 %collective-permute-start.1 = (f32[168,128]{1,0:T(8,128)}, f32[168,128]{1,0:T(8,128)S(1)}, u32[]{:S(2)}, u32[]{:S(2)}) collective-permute-start(f32[168,128]{1,0:T(8,128)} %get-tuple-element.73), channel_id=1, source_target_pairs={{0,2},{1,3},{2,0},{3,1},{4,6},{5,7},{6,4},{7,5},{8,10},{9,11},{10,... | collective-permute-start | bytes 258056 | tf_op jit(solution)/shard_map/ppermute | solution.py:604
  73.5 29.7 %collective-permute-start.2 = (f32[168,128]{1,0:T(8,128)}, f32[168,128]{1,0:T(8,128)S(1)}, u32[]{:S(2)}, u32[]{:S(2)}) collective-permute-start(f32[168,128]{1,0:T(8,128)} %get-tuple-element.74), channel_id=1, source_target_pairs={{0,3},{1,2},{2,1},{3,0},{4,7},{5,6},{6,5},{7,4},{8,11},{9,10},{10,... | collective-permute-start | bytes 258056 | tf_op jit(solution)/shard_map/ppermute | solution.py:604
  74.0 43.5 %collective-permute-start.3 = (f32[168,128]{1,0:T(8,128)}, f32[168,128]{1,0:T(8,128)S(1)}, u32[]{:S(2)}, u32[]{:S(2)}) collective-permute-start(f32[168,128]{1,0:T(8,128)} %get-tuple-element.75), channel_id=1, source_target_pairs={{0,4},{1,5},{2,6},{3,7},{4,0},{5,1},{6,2},{7,3},{8,12},{9,13},{10,... | collective-permute-start | bytes 258056 | tf_op jit(solution)/shard_map/ppermute | solution.py:604
  76.5 43.8 %collective-permute-start.4 = (f32[168,128]{1,0:T(8,128)}, f32[168,128]{1,0:T(8,128)S(1)}, u32[]{:S(2)}, u32[]{:S(2)}) collective-permute-start(f32[168,128]{1,0:T(8,128)} %get-tuple-element.76), channel_id=1, source_target_pairs={{0,5},{1,4},{2,7},{3,6},{4,1},{5,0},{6,3},{7,2},{8,13},{9,12},{10,... | collective-permute-start | bytes 258056 | tf_op jit(solution)/shard_map/ppermute | solution.py:604
  88.5 31.8 %collective-permute-start.5 = (f32[168,128]{1,0:T(8,128)}, f32[168,128]{1,0:T(8,128)S(1)}, u32[]{:S(2)}, u32[]{:S(2)}) collective-permute-start(f32[168,128]{1,0:T(8,128)} %get-tuple-element.77), channel_id=1, source_target_pairs={{0,6},{1,7},{2,4},{3,5},{4,2},{5,3},{6,0},{7,1},{8,14},{9,15},{10,... | collective-permute-start | bytes 258056 | tf_op jit(solution)/shard_map/ppermute | solution.py:604
  98.7 23.3 %collective-permute-start.6 = (f32[168,128]{1,0:T(8,128)}, f32[168,128]{1,0:T(8,128)S(1)}, u32[]{:S(2)}, u32[]{:S(2)}) collective-permute-start(f32[168,128]{1,0:T(8,128)} %get-tuple-element.78), channel_id=1, source_target_pairs={{0,7},{1,6},{2,5},{3,4},{4,3},{5,2},{6,1},{7,0},{8,15},{9,14},{10,... | collective-permute-start | bytes 258056 | tf_op jit(solution)/shard_map/ppermute | solution.py:604
  103.2 20.2 %collective-permute-start.7 = (f32[168,128]{1,0:T(8,128)}, f32[168,128]{1,0:T(8,128)S(1)}, u32[]{:S(2)}, u32[]{:S(2)}) collective-permute-start(f32[168,128]{1,0:T(8,128)} %get-tuple-element.79), channel_id=1, source_target_pairs={{0,8},{1,9},{2,10},{3,11},{4,12},{5,13},{6,14},{7,15},{8,0},{9,1},... | collective-permute-start | bytes 258056 | tf_op jit(solution)/shard_map/ppermute | solution.py:604
  117.5 8.3 %collective-permute-start.8 = (f32[168,128]{1,0:T(8,128)S(1)}, f32[168,128]{1,0:T(8,128)S(1)}, u32[]{:S(2)}, u32[]{:S(2)}) collective-permute-start(f32[168,128]{1,0:T(8,128)S(1)} %copy-done.81), channel_id=1, source_target_pairs={{0,9},{1,8},{2,11},{3,10},{4,13},{5,12},{6,15},{7,14},{8,1},{9,0},... | collective-permute-start | bytes 258056 | tf_op jit(solution)/shard_map/ppermute | solution.py:604
  120.2 6.0 %collective-permute-start.9 = (f32[168,128]{1,0:T(8,128)S(1)}, f32[168,128]{1,0:T(8,128)S(1)}, u32[]{:S(2)}, u32[]{:S(2)}) collective-permute-start(f32[168,128]{1,0:T(8,128)S(1)} %copy-done.80), channel_id=1, source_target_pairs={{0,10},{1,11},{2,8},{3,9},{4,14},{5,15},{6,12},{7,13},{8,2},{9,3},... | collective-permute-start | bytes 258056 | tf_op jit(solution)/shard_map/ppermute | solution.py:604
  120.3 9.1 %collective-permute-start.10 = (f32[168,128]{1,0:T(8,128)S(1)}, f32[168,128]{1,0:T(8,128)S(1)}, u32[]{:S(2)}, u32[]{:S(2)}) collective-permute-start(f32[168,128]{1,0:T(8,128)S(1)} %copy-done.79), channel_id=1, source_target_pairs={{0,11},{1,10},{2,9},{3,8},{4,15},{5,14},{6,13},{7,12},{8,3},{9,2},... | collective-permute-start | bytes 258056 | tf_op jit(solution)/shard_map/ppermute | solution.py:604
  122.0 8.9 %collective-permute-start.11 = (f32[168,128]{1,0:T(8,128)S(1)}, f32[168,128]{1,0:T(8,128)S(1)}, u32[]{:S(2)}, u32[]{:S(2)}) collective-permute-start(f32[168,128]{1,0:T(8,128)S(1)} %copy-done.78), channel_id=1, source_target_pairs={{0,12},{1,13},{2,14},{3,15},{4,8},{5,9},{6,10},{7,11},{8,4},{9,5},... | collective-permute-start | bytes 258056 | tf_op jit(solution)/shard_map/ppermute | solution.py:604
  123.5 14.5 %collective-permute-start.12 = (f32[168,128]{1,0:T(8,128)S(1)}, f32[168,128]{1,0:T(8,128)S(1)}, u32[]{:S(2)}, u32[]{:S(2)}) collective-permute-start(f32[168,128]{1,0:T(8,128)S(1)} %copy-done.77), channel_id=1, source_target_pairs={{0,13},{1,12},{2,15},{3,14},{4,9},{5,8},{6,11},{7,10},{8,5},{9,4},... | collective-permute-start | bytes 258056 | tf_op jit(solution)/shard_map/ppermute | solution.py:604
  125.7 12.2 %collective-permute-start.13 = (f32[168,128]{1,0:T(8,128)S(1)}, f32[168,128]{1,0:T(8,128)S(1)}, u32[]{:S(2)}, u32[]{:S(2)}) collective-permute-start(f32[168,128]{1,0:T(8,128)S(1)} %copy-done.76), channel_id=1, source_target_pairs={{0,14},{1,15},{2,12},{3,13},{4,10},{5,11},{6,8},{7,9},{8,6},{9,7},... | collective-permute-start | bytes 258056 | tf_op jit(solution)/shard_map/ppermute | solution.py:604
  126.2 15.1 %collective-permute-start.14 = (f32[168,128]{1,0:T(8,128)S(1)}, f32[168,128]{1,0:T(8,128)S(1)}, u32[]{:S(2)}, u32[]{:S(2)}) collective-permute-start(f32[168,128]{1,0:T(8,128)S(1)} %copy-done.75), channel_id=1, source_target_pairs={{0,15},{1,14},{2,13},{3,12},{4,11},{5,10},{6,9},{7,8},{8,7},{9,6},... | collective-permute-start | bytes 258056 | tf_op jit(solution)/shard_map/ppermute | solution.py:604
  129.4 13.8 %collective-permute-start.15 = (f32[168,128]{1,0:T(8,128)S(1)}, f32[168,128]{1,0:T(8,128)S(1)}, u32[]{:S(2)}, u32[]{:S(2)}) collective-permute-start(f32[168,128]{1,0:T(8,128)S(1)} %copy-done.74), channel_id=1, source_target_pairs={{0,16},{1,17},{2,18},{3,19},{4,20},{5,21},{6,22},{7,23},{8,24},{9,... | collective-permute-start | bytes 258056 | tf_op jit(solution)/shard_map/ppermute | solution.py:604
  130.9 14.9 %collective-permute-start.16 = (f32[168,128]{1,0:T(8,128)S(1)}, f32[168,128]{1,0:T(8,128)S(1)}, u32[]{:S(2)}, u32[]{:S(2)}) collective-permute-start(f32[168,128]{1,0:T(8,128)S(1)} %copy-done.73), channel_id=1, source_target_pairs={{0,17},{1,16},{2,19},{3,18},{4,21},{5,20},{6,23},{7,22},{8,25},{9,... | collective-permute-start | bytes 258056 | tf_op jit(solution)/shard_map/ppermute | solution.py:604
  138.0 9.5 %collective-permute-start.17 = (f32[168,128]{1,0:T(8,128)S(1)}, f32[168,128]{1,0:T(8,128)S(1)}, u32[]{:S(2)}, u32[]{:S(2)}) collective-permute-start(f32[168,128]{1,0:T(8,128)S(1)} %copy-done.72), channel_id=1, source_target_pairs={{0,18},{1,19},{2,16},{3,17},{4,22},{5,23},{6,20},{7,21},{8,26},{9,... | collective-permute-start | bytes 258056 | tf_op jit(solution)/shard_map/ppermute | solution.py:604
  138.0 13.0 %collective-permute-start.18 = (f32[168,128]{1,0:T(8,128)S(1)}, f32[168,128]{1,0:T(8,128)S(1)}, u32[]{:S(2)}, u32[]{:S(2)}) collective-permute-start(f32[168,128]{1,0:T(8,128)S(1)} %copy-done.71), channel_id=1, source_target_pairs={{0,19},{1,18},{2,17},{3,16},{4,23},{5,22},{6,21},{7,20},{8,27},{9,... | collective-permute-start | bytes 258056 | tf_op jit(solution)/shard_map/ppermute | solution.py:604
  141.3 14.2 %collective-permute-start.19 = (f32[168,128]{1,0:T(8,128)S(1)}, f32[168,128]{1,0:T(8,128)S(1)}, u32[]{:S(2)}, u32[]{:S(2)}) collective-permute-start(f32[168,128]{1,0:T(8,128)S(1)} %copy-done.70), channel_id=1, source_target_pairs={{0,20},{1,21},{2,22},{3,23},{4,16},{5,17},{6,18},{7,19},{8,28},{9,... | collective-permute-start | bytes 258056 | tf_op jit(solution)/shard_map/ppermute | solution.py:604
  143.2 14.1 %collective-permute-start.20 = (f32[168,128]{1,0:T(8,128)S(1)}, f32[168,128]{1,0:T(8,128)S(1)}, u32[]{:S(2)}, u32[]{:S(2)}) collective-permute-start(f32[168,128]{1,0:T(8,128)S(1)} %copy-done.69), channel_id=1, source_target_pairs={{0,21},{1,20},{2,23},{3,22},{4,17},{5,16},{6,19},{7,18},{8,29},{9,... | collective-permute-start | bytes 258056 | tf_op jit(solution)/shard_map/ppermute | solution.py:604
  145.8 11.5 %collective-permute-start.21 = (f32[168,128]{1,0:T(8,128)S(1)}, f32[168,128]{1,0:T(8,128)S(1)}, u32[]{:S(2)}, u32[]{:S(2)}) collective-permute-start(f32[168,128]{1,0:T(8,128)S(1)} %copy-done.68), channel_id=1, source_target_pairs={{0,22},{1,23},{2,20},{3,21},{4,18},{5,19},{6,16},{7,17},{8,30},{9,... | collective-permute-start | bytes 258056 | tf_op jit(solution)/shard_map/ppermute | solution.py:604
  147.4 13.4 %collective-permute-start.22 = (f32[168,128]{1,0:T(8,128)S(1)}, f32[168,128]{1,0:T(8,128)S(1)}, u32[]{:S(2)}, u32[]{:S(2)}) collective-permute-start(f32[168,128]{1,0:T(8,128)S(1)} %copy-done.67), channel_id=1, source_target_pairs={{0,23},{1,22},{2,21},{3,20},{4,19},{5,18},{6,17},{7,16},{8,31},{9,... | collective-permute-start | bytes 258056 | tf_op jit(solution)/shard_map/ppermute | solution.py:604
  151.0 10.2 %collective-permute-start.23 = (f32[168,128]{1,0:T(8,128)S(1)}, f32[168,128]{1,0:T(8,128)S(1)}, u32[]{:S(2)}, u32[]{:S(2)}) collective-permute-start(f32[168,128]{1,0:T(8,128)S(1)} %copy-done.66), channel_id=1, source_target_pairs={{0,24},{1,25},{2,26},{3,27},{4,28},{5,29},{6,30},{7,31},{8,16},{9,... | collective-permute-start | bytes 258056 | tf_op jit(solution)/shard_map/ppermute | solution.py:604
  155.5 9.1 %collective-permute-start.24 = (f32[168,128]{1,0:T(8,128)S(1)}, f32[168,128]{1,0:T(8,128)S(1)}, u32[]{:S(2)}, u32[]{:S(2)}) collective-permute-start(f32[168,128]{1,0:T(8,128)S(1)} %copy-done.65), channel_id=1, source_target_pairs={{0,25},{1,24},{2,27},{3,26},{4,29},{5,28},{6,31},{7,30},{8,17},{9,... | collective-permute-start | bytes 258056 | tf_op jit(solution)/shard_map/ppermute | solution.py:604
  157.3 8.3 %collective-permute-start.25 = (f32[168,128]{1,0:T(8,128)S(1)}, f32[168,128]{1,0:T(8,128)S(1)}, u32[]{:S(2)}, u32[]{:S(2)}) collective-permute-start(f32[168,128]{1,0:T(8,128)S(1)} %copy-done.64), channel_id=1, source_target_pairs={{0,26},{1,27},{2,24},{3,25},{4,30},{5,31},{6,28},{7,29},{8,18},{9,... | collective-permute-start | bytes 258056 | tf_op jit(solution)/shard_map/ppermute | solution.py:604
  157.4 12.6 %collective-permute-start.26 = (f32[168,128]{1,0:T(8,128)S(1)}, f32[168,128]{1,0:T(8,128)S(1)}, u32[]{:S(2)}, u32[]{:S(2)}) collective-permute-start(f32[168,128]{1,0:T(8,128)S(1)} %copy-done.63), channel_id=1, source_target_pairs={{0,27},{1,26},{2,25},{3,24},{4,31},{5,30},{6,29},{7,28},{8,19},{9,... | collective-permute-start | bytes 258056 | tf_op jit(solution)/shard_map/ppermute | solution.py:604
  160.9 14.1 %collective-permute-start.27 = (f32[168,128]{1,0:T(8,128)S(1)}, f32[168,128]{1,0:T(8,128)S(1)}, u32[]{:S(2)}, u32[]{:S(2)}) collective-permute-start(f32[168,128]{1,0:T(8,128)S(1)} %copy-done.62), channel_id=1, source_target_pairs={{0,28},{1,29},{2,30},{3,31},{4,24},{5,25},{6,26},{7,27},{8,20},{9,... | collective-permute-start | bytes 258056 | tf_op jit(solution)/shard_map/ppermute | solution.py:604
  161.2 15.4 %collective-permute-start.28 = (f32[168,128]{1,0:T(8,128)S(1)}, f32[168,128]{1,0:T(8,128)S(1)}, u32[]{:S(2)}, u32[]{:S(2)}) collective-permute-start(f32[168,128]{1,0:T(8,128)S(1)} %copy-done.61), channel_id=1, source_target_pairs={{0,29},{1,28},{2,31},{3,30},{4,25},{5,24},{6,27},{7,26},{8,21},{9,... | collective-permute-start | bytes 258056 | tf_op jit(solution)/shard_map/ppermute | solution.py:604
  164.6 12.0 %collective-permute-start.29 = (f32[168,128]{1,0:T(8,128)S(1)}, f32[168,128]{1,0:T(8,128)S(1)}, u32[]{:S(2)}, u32[]{:S(2)}) collective-permute-start(f32[168,128]{1,0:T(8,128)S(1)} %copy-done.60), channel_id=1, source_target_pairs={{0,30},{1,31},{2,28},{3,29},{4,26},{5,27},{6,24},{7,25},{8,22},{9,... | collective-permute-start | bytes 258056 | tf_op jit(solution)/shard_map/ppermute | solution.py:604
  165.7 10.9 %collective-permute-start.30 = (f32[168,128]{1,0:T(8,128)S(1)}, f32[168,128]{1,0:T(8,128)S(1)}, u32[]{:S(2)}, u32[]{:S(2)}) collective-permute-start(f32[168,128]{1,0:T(8,128)S(1)} %copy-done.59), channel_id=1, source_target_pairs={{0,31},{1,30},{2,29},{3,28},{4,27},{5,26},{6,25},{7,24},{8,23},{9,... | collective-permute-start | bytes 258056 | tf_op jit(solution)/shard_map/ppermute | solution.py:604
  191.3 9.5 %collective-permute-start.31 = (f32[168,128]{1,0:T(8,128)}, f32[168,128]{1,0:T(8,128)S(1)}, u32[]{:S(2)}, u32[]{:S(2)}) collective-permute-start(f32[168,128]{1,0:T(8,128)} %get-tuple-element.104), channel_id=1, source_target_pairs={{0,1},{1,0},{2,3},{3,2},{4,5},{5,4},{6,7},{7,6},{8,9},{9,8},{10,11... | collective-permute-start | bytes 258056 | tf_op jit(solution)/shard_map/ppermute | solution.py:604
  193.0 9.3 %collective-permute-start.32 = (f32[168,128]{1,0:T(8,128)}, f32[168,128]{1,0:T(8,128)S(1)}, u32[]{:S(2)}, u32[]{:S(2)}) collective-permute-start(f32[168,128]{1,0:T(8,128)} %get-tuple-element.105), channel_id=1, source_target_pairs={{0,2},{1,3},{2,0},{3,1},{4,6},{5,7},{6,4},{7,5},{8,10},{9,11},{10,... | collective-permute-start | bytes 258056 | tf_op jit(solution)/shard_map/ppermute | solution.py:604
  196.9 7.7 %collective-permute-start.33 = (f32[168,128]{1,0:T(8,128)}, f32[168,128]{1,0:T(8,128)S(1)}, u32[]{:S(2)}, u32[]{:S(2)}) collective-permute-start(f32[168,128]{1,0:T(8,128)} %get-tuple-element.106), channel_id=1, source_target_pairs={{0,3},{1,2},{2,1},{3,0},{4,7},{5,6},{6,5},{7,4},{8,11},{9,10},{10,... | collective-permute-start | bytes 258056 | tf_op jit(solution)/shard_map/ppermute | solution.py:604
  197.0 13.7 %collective-permute-start.34 = (f32[168,128]{1,0:T(8,128)}, f32[168,128]{1,0:T(8,128)S(1)}, u32[]{:S(2)}, u32[]{:S(2)}) collective-permute-start(f32[168,128]{1,0:T(8,128)} %get-tuple-element.107), channel_id=1, source_target_pairs={{0,4},{1,5},{2,6},{3,7},{4,0},{5,1},{6,2},{7,3},{8,12},{9,13},{10,... | collective-permute-start | bytes 258056 | tf_op jit(solution)/shard_map/ppermute | solution.py:604
  198.3 15.0 %collective-permute-start.35 = (f32[168,128]{1,0:T(8,128)}, f32[168,128]{1,0:T(8,128)S(1)}, u32[]{:S(2)}, u32[]{:S(2)}) collective-permute-start(f32[168,128]{1,0:T(8,128)} %get-tuple-element.108), channel_id=1, source_target_pairs={{0,5},{1,4},{2,7},{3,6},{4,1},{5,0},{6,3},{7,2},{8,13},{9,12},{10,... | collective-permute-start | bytes 258056 | tf_op jit(solution)/shard_map/ppermute | solution.py:604
  200.8 12.6 %collective-permute-start.36 = (f32[168,128]{1,0:T(8,128)}, f32[168,128]{1,0:T(8,128)S(1)}, u32[]{:S(2)}, u32[]{:S(2)}) collective-permute-start(f32[168,128]{1,0:T(8,128)} %get-tuple-element.109), channel_id=1, source_target_pairs={{0,6},{1,7},{2,4},{3,5},{4,2},{5,3},{6,0},{7,1},{8,14},{9,15},{10,... | collective-permute-start | bytes 258056 | tf_op jit(solution)/shard_map/ppermute | solution.py:604
  202.2 13.0 %collective-permute-start.37 = (f32[168,128]{1,0:T(8,128)}, f32[168,128]{1,0:T(8,128)S(1)}, u32[]{:S(2)}, u32[]{:S(2)}) collective-permute-start(f32[168,128]{1,0:T(8,128)} %get-tuple-element.110), channel_id=1, source_target_pairs={{0,7},{1,6},{2,5},{3,4},{4,3},{5,2},{6,1},{7,0},{8,15},{9,14},{10,... | collective-permute-start | bytes 258056 | tf_op jit(solution)/shard_map/ppermute | solution.py:604
  204.6 11.6 %collective-permute-start.38 = (f32[168,128]{1,0:T(8,128)}, f32[168,128]{1,0:T(8,128)S(1)}, u32[]{:S(2)}, u32[]{:S(2)}) collective-permute-start(f32[168,128]{1,0:T(8,128)} %get-tuple-element.111), channel_id=1, source_target_pairs={{0,8},{1,9},{2,10},{3,11},{4,12},{5,13},{6,14},{7,15},{8,0},{9,1},... | collective-permute-start | bytes 258056 | tf_op jit(solution)/shard_map/ppermute | solution.py:604
  210.7 8.0 %collective-permute-start.39 = (f32[168,128]{1,0:T(8,128)}, f32[168,128]{1,0:T(8,128)S(1)}, u32[]{:S(2)}, u32[]{:S(2)}) collective-permute-start(f32[168,128]{1,0:T(8,128)} %get-tuple-element.112), channel_id=1, source_target_pairs={{0,9},{1,8},{2,11},{3,10},{4,13},{5,12},{6,15},{7,14},{8,1},{9,0},... | collective-permute-start | bytes 258056 | tf_op jit(solution)/shard_map/ppermute | solution.py:604
  213.4 6.5 %collective-permute-start.40 = (f32[168,128]{1,0:T(8,128)}, f32[168,128]{1,0:T(8,128)S(1)}, u32[]{:S(2)}, u32[]{:S(2)}) collective-permute-start(f32[168,128]{1,0:T(8,128)} %get-tuple-element.113), channel_id=1, source_target_pairs={{0,10},{1,11},{2,8},{3,9},{4,14},{5,15},{6,12},{7,13},{8,2},{9,3},... | collective-permute-start | bytes 258056 | tf_op jit(solution)/shard_map/ppermute | solution.py:604
  213.4 8.9 %collective-permute-start.41 = (f32[168,128]{1,0:T(8,128)}, f32[168,128]{1,0:T(8,128)S(1)}, u32[]{:S(2)}, u32[]{:S(2)}) collective-permute-start(f32[168,128]{1,0:T(8,128)} %get-tuple-element.114), channel_id=1, source_target_pairs={{0,11},{1,10},{2,9},{3,8},{4,15},{5,14},{6,13},{7,12},{8,3},{9,2},... | collective-permute-start | bytes 258056 | tf_op jit(solution)/shard_map/ppermute | solution.py:604
  215.2 12.6 %collective-permute-start.42 = (f32[168,128]{1,0:T(8,128)}, f32[168,128]{1,0:T(8,128)S(1)}, u32[]{:S(2)}, u32[]{:S(2)}) collective-permute-start(f32[168,128]{1,0:T(8,128)} %get-tuple-element.115), channel_id=1, source_target_pairs={{0,12},{1,13},{2,14},{3,15},{4,8},{5,9},{6,10},{7,11},{8,4},{9,5},... | collective-permute-start | bytes 258056 | tf_op jit(solution)/shard_map/ppermute | solution.py:604
  216.2 14.8 %collective-permute-start.43 = (f32[168,128]{1,0:T(8,128)}, f32[168,128]{1,0:T(8,128)S(1)}, u32[]{:S(2)}, u32[]{:S(2)}) collective-permute-start(f32[168,128]{1,0:T(8,128)} %get-tuple-element.116), channel_id=1, source_target_pairs={{0,13},{1,12},{2,15},{3,14},{4,9},{5,8},{6,11},{7,10},{8,5},{9,4},... | collective-permute-start | bytes 258056 | tf_op jit(solution)/shard_map/ppermute | solution.py:604
  218.7 12.4 %collective-permute-start.44 = (f32[168,128]{1,0:T(8,128)}, f32[168,128]{1,0:T(8,128)S(1)}, u32[]{:S(2)}, u32[]{:S(2)}) collective-permute-start(f32[168,128]{1,0:T(8,128)} %get-tuple-element.117), channel_id=1, source_target_pairs={{0,14},{1,15},{2,12},{3,13},{4,10},{5,11},{6,8},{7,9},{8,6},{9,7},... | collective-permute-start | bytes 258056 | tf_op jit(solution)/shard_map/ppermute | solution.py:604
  219.9 13.6 %collective-permute-start.45 = (f32[168,128]{1,0:T(8,128)}, f32[168,128]{1,0:T(8,128)S(1)}, u32[]{:S(2)}, u32[]{:S(2)}) collective-permute-start(f32[168,128]{1,0:T(8,128)} %get-tuple-element.118), channel_id=1, source_target_pairs={{0,15},{1,14},{2,13},{3,12},{4,11},{5,10},{6,9},{7,8},{8,7},{9,6},... | collective-permute-start | bytes 258056 | tf_op jit(solution)/shard_map/ppermute | solution.py:604
  222.3 14.0 %collective-permute-start.46 = (f32[168,128]{1,0:T(8,128)}, f32[168,128]{1,0:T(8,128)S(1)}, u32[]{:S(2)}, u32[]{:S(2)}) collective-permute-start(f32[168,128]{1,0:T(8,128)} %get-tuple-element.119), channel_id=1, source_target_pairs={{0,16},{1,17},{2,18},{3,19},{4,20},{5,21},{6,22},{7,23},{8,24},{9,... | collective-permute-start | bytes 258056 | tf_op jit(solution)/shard_map/ppermute | solution.py:604
  227.8 10.9 %collective-permute-start.47 = (f32[168,128]{1,0:T(8,128)}, f32[168,128]{1,0:T(8,128)S(1)}, u32[]{:S(2)}, u32[]{:S(2)}) collective-permute-start(f32[168,128]{1,0:T(8,128)} %get-tuple-element.120), channel_id=1, source_target_pairs={{0,17},{1,16},{2,19},{3,18},{4,21},{5,20},{6,23},{7,22},{8,25},{9,... | collective-permute-start | bytes 258056 | tf_op jit(solution)/shard_map/ppermute | solution.py:604
  231.0 10.0 %collective-permute-start.48 = (f32[168,128]{1,0:T(8,128)}, f32[168,128]{1,0:T(8,128)S(1)}, u32[]{:S(2)}, u32[]{:S(2)}) collective-permute-start(f32[168,128]{1,0:T(8,128)} %get-tuple-element.121), channel_id=1, source_target_pairs={{0,18},{1,19},{2,16},{3,17},{4,22},{5,23},{6,20},{7,21},{8,26},{9,... | collective-permute-start | bytes 258056 | tf_op jit(solution)/shard_map/ppermute | solution.py:604
  231.1 11.9 %collective-permute-start.49 = (f32[168,128]{1,0:T(8,128)}, f32[168,128]{1,0:T(8,128)S(1)}, u32[]{:S(2)}, u32[]{:S(2)}) collective-permute-start(f32[168,128]{1,0:T(8,128)} %get-tuple-element.122), channel_id=1, source_target_pairs={{0,19},{1,18},{2,17},{3,16},{4,23},{5,22},{6,21},{7,20},{8,27},{9,... | collective-permute-start | bytes 258056 | tf_op jit(solution)/shard_map/ppermute | solution.py:604
  233.5 14.0 %collective-permute-start.50 = (f32[168,128]{1,0:T(8,128)}, f32[168,128]{1,0:T(8,128)S(1)}, u32[]{:S(2)}, u32[]{:S(2)}) collective-permute-start(f32[168,128]{1,0:T(8,128)} %get-tuple-element.123), channel_id=1, source_target_pairs={{0,20},{1,21},{2,22},{3,23},{4,16},{5,17},{6,18},{7,19},{8,28},{9,... | collective-permute-start | bytes 258056 | tf_op jit(solution)/shard_map/ppermute | solution.py:604
  236.3 14.7 %collective-permute-start.51 = (f32[168,128]{1,0:T(8,128)}, f32[168,128]{1,0:T(8,128)S(1)}, u32[]{:S(2)}, u32[]{:S(2)}) collective-permute-start(f32[168,128]{1,0:T(8,128)} %get-tuple-element.124), channel_id=1, source_target_pairs={{0,21},{1,20},{2,23},{3,22},{4,17},{5,16},{6,19},{7,18},{8,29},{9,... | collective-permute-start | bytes 258056 | tf_op jit(solution)/shard_map/ppermute | solution.py:604
  238.7 12.4 %collective-permute-start.52 = (f32[168,128]{1,0:T(8,128)}, f32[168,128]{1,0:T(8,128)S(1)}, u32[]{:S(2)}, u32[]{:S(2)}) collective-permute-start(f32[168,128]{1,0:T(8,128)} %get-tuple-element.125), channel_id=1, source_target_pairs={{0,22},{1,23},{2,20},{3,21},{4,18},{5,19},{6,16},{7,17},{8,30},{9,... | collective-permute-start | bytes 258056 | tf_op jit(solution)/shard_map/ppermute | solution.py:604
  241.1 12.6 %collective-permute-start.53 = (f32[168,128]{1,0:T(8,128)}, f32[168,128]{1,0:T(8,128)S(1)}, u32[]{:S(2)}, u32[]{:S(2)}) collective-permute-start(f32[168,128]{1,0:T(8,128)} %get-tuple-element.126), channel_id=1, source_target_pairs={{0,23},{1,22},{2,21},{3,20},{4,19},{5,18},{6,17},{7,16},{8,31},{9,... | collective-permute-start | bytes 258056 | tf_op jit(solution)/shard_map/ppermute | solution.py:604
  243.0 11.5 %collective-permute-start.54 = (f32[168,128]{1,0:T(8,128)}, f32[168,128]{1,0:T(8,128)S(1)}, u32[]{:S(2)}, u32[]{:S(2)}) collective-permute-start(f32[168,128]{1,0:T(8,128)} %get-tuple-element.127), channel_id=1, source_target_pairs={{0,24},{1,25},{2,26},{3,27},{4,28},{5,29},{6,30},{7,31},{8,16},{9,... | collective-permute-start | bytes 258056 | tf_op jit(solution)/shard_map/ppermute | solution.py:604
  247.5 10.7 %collective-permute-start.55 = (f32[168,128]{1,0:T(8,128)}, f32[168,128]{1,0:T(8,128)S(1)}, u32[]{:S(2)}, u32[]{:S(2)}) collective-permute-start(f32[168,128]{1,0:T(8,128)} %get-tuple-element.128), channel_id=1, source_target_pairs={{0,25},{1,24},{2,27},{3,26},{4,29},{5,28},{6,31},{7,30},{8,17},{9,... | collective-permute-start | bytes 258056 | tf_op jit(solution)/shard_map/ppermute | solution.py:604
  251.1 8.8 %collective-permute-start.56 = (f32[168,128]{1,0:T(8,128)}, f32[168,128]{1,0:T(8,128)S(1)}, u32[]{:S(2)}, u32[]{:S(2)}) collective-permute-start(f32[168,128]{1,0:T(8,128)} %get-tuple-element.129), channel_id=1, source_target_pairs={{0,26},{1,27},{2,24},{3,25},{4,30},{5,31},{6,28},{7,29},{8,18},{9,... | collective-permute-start | bytes 258056 | tf_op jit(solution)/shard_map/ppermute | solution.py:604
  251.1 14.5 %collective-permute-start.57 = (f32[168,128]{1,0:T(8,128)}, f32[168,128]{1,0:T(8,128)}, u32[]{:S(2)}, u32[]{:S(2)}) collective-permute-start(f32[168,128]{1,0:T(8,128)} %get-tuple-element.130), channel_id=1, source_target_pairs={{0,27},{1,26},{2,25},{3,24},{4,31},{5,30},{6,29},{7,28},{8,19},{9,... | collective-permute-start | bytes 258056 | tf_op jit(solution)/shard_map/ppermute | solution.py:604
  253.7 11.9 %collective-permute-start.58 = (f32[168,128]{1,0:T(8,128)}, f32[168,128]{1,0:T(8,128)}, u32[]{:S(2)}, u32[]{:S(2)}) collective-permute-start(f32[168,128]{1,0:T(8,128)} %get-tuple-element.131), channel_id=1, source_target_pairs={{0,28},{1,29},{2,30},{3,31},{4,24},{5,25},{6,26},{7,27},{8,20},{9,... | collective-permute-start | bytes 258056 | tf_op jit(solution)/shard_map/ppermute | solution.py:604
  254.4 16.2 %collective-permute-start.59 = (f32[168,128]{1,0:T(8,128)}, f32[168,128]{1,0:T(8,128)}, u32[]{:S(2)}, u32[]{:S(2)}) collective-permute-start(f32[168,128]{1,0:T(8,128)} %get-tuple-element.132), channel_id=1, source_target_pairs={{0,29},{1,28},{2,31},{3,30},{4,25},{5,24},{6,27},{7,26},{8,21},{9,... | collective-permute-start | bytes 258056 | tf_op jit(solution)/shard_map/ppermute | solution.py:604
  258.2 12.5 %collective-permute-start.60 = (f32[168,128]{1,0:T(8,128)}, f32[168,128]{1,0:T(8,128)}, u32[]{:S(2)}, u32[]{:S(2)}) collective-permute-start(f32[168,128]{1,0:T(8,128)} %get-tuple-element.133), channel_id=1, source_target_pairs={{0,30},{1,31},{2,28},{3,29},{4,26},{5,27},{6,24},{7,25},{8,22},{9,... | collective-permute-start | bytes 258056 | tf_op jit(solution)/shard_map/ppermute | solution.py:604
  260.5 10.2 %collective-permute-start.61 = (f32[168,128]{1,0:T(8,128)}, f32[168,128]{1,0:T(8,128)}, u32[]{:S(2)}, u32[]{:S(2)}) collective-permute-start(f32[168,128]{1,0:T(8,128)} %get-tuple-element.134), channel_id=1, source_target_pairs={{0,31},{1,30},{2,29},{3,28},{4,27},{5,26},{6,25},{7,24},{8,23},{9,... | collective-permute-start | bytes 258056 | tf_op jit(solution)/shard_map/ppermute | solution.py:604
  (82 other events, 3782.1 us)
